TPU v7x, 32 devices: a whole 2x2x4 slice. The times are simulated.
32 devices in a mesh: seq: 16 (over z, y, core), ch: 2 (over x).
Axes of the slice: x: 2, y: 2, z: 4, core: 2. Of those that a mesh axis runs over, the one named last changes fastest.
Arguments:
- query_gate: bfloat16 [2, 2048, 2048], P('ch', 'seq'), may hold values from -6 to 6
- key_input: bfloat16 [2, 2048, 2048], P('ch', 'seq'), may hold values from -6 to 6
- value_input: bfloat16 [2, 2048, 2048], P('ch', 'seq'), may hold values from -6 to 6
- grad_output: bfloat16 [2, 2048, 2048], P('ch', 'seq'), may hold values from -6 to 6
- filter_raw: bfloat16 [2048, 2048], P('seq'), may hold values from -6 to 6
- skip_gain: float32 [2048], replicated, may hold values from 0.5 to 1.5
Outputs:
- grad_query: bfloat16 [2, 2048, 2048], P('ch', 'seq')
- grad_key: bfloat16 [2, 2048, 2048], P('ch', 'seq')
- grad_value: bfloat16 [2, 2048, 2048], P('ch', 'seq')
- grad_filter: float32 [2048, 2048], P('seq', 'ch')
All inputs are finite; a program needn't handle non-finite values.
Results may differ from a plain program's by a relative error of at most 0.001.
Values sent between devices are 32-bit elements; how exact they have to be, the bound alone decides.
A program may use at most 128 MiB of HBM per device.

v0:
```python
import math

import numpy as np

import jax
import jax.numpy as jnp
from jax import lax
from jax.experimental import pallas as pl
from jax.experimental.pallas import tpu as pltpu
from jax.sharding import PartitionSpec as P


def angle_table(row_index, col_index, modulus):
    turn_count = row_index[:, None] * col_index[None, :] % modulus
    angles = turn_count.astype(jnp.float32) * (2.0 * math.pi / modulus)
    return (jnp.cos(angles), jnp.sin(angles))


def contract(pattern, table, operand):
    return jnp.einsum(
        pattern, table, operand, precision=lax.Precision.HIGHEST, preferred_element_type=jnp.float32
    )


def rotate(pattern, cos_table, sin_table, sense_sign, real_part, imag_part, want_imag):
    if imag_part is None:
        cos_term = contract(pattern, cos_table, real_part)
        return (cos_term, sense_sign * contract(pattern, sin_table, real_part))
    real_out = contract(pattern, cos_table, real_part) - sense_sign * contract(
        pattern, sin_table, imag_part
    )
    if not want_imag:
        return (real_out, None)
    imag_out = contract(pattern, cos_table, imag_part) + sense_sign * contract(
        pattern, sin_table, real_part
    )
    return (real_out, imag_out)


def twist(cos_table, sin_table, sense_sign, real_part, imag_part):
    return (
        real_part * cos_table - sense_sign * imag_part * sin_table,
        imag_part * cos_table + sense_sign * real_part * sin_table,
    )


def spectral_terms(z_real, z_imag, g_real, g_imag, h_real, h_imag):
    conv_real = z_real * h_real - z_imag * h_imag
    conv_imag = z_real * h_imag + z_imag * h_real
    back_real = h_real * g_real + h_imag * g_imag
    back_imag = h_real * g_imag - h_imag * g_real
    corr_real = z_real * g_real + z_imag * g_imag
    corr_imag = z_real * g_imag - z_imag * g_real
    return (conv_real - back_imag, conv_imag + back_real, corr_real, corr_imag)


def shards(query_gate, key_input, value_input, grad_output, filter_raw, skip_gain):
    seq_count = lax.axis_size("seq")
    key_f = key_input[0].astype(jnp.float32)
    value_f = value_input[0].astype(jnp.float32)
    out_f = grad_output[0].astype(jnp.float32)
    mixed = key_f * value_f
    gated = out_f * query_gate[0].astype(jnp.float32)
    tokens, channels = mixed.shape
    seq_length = tokens * seq_count
    full_length = 2 * seq_length
    inverse_scale = 1.0 / full_length
    filter_taps = filter_raw.astype(jnp.float32) * seq_length ** (-0.5)
    freq_one = jnp.arange(2 * seq_count, dtype=jnp.int32)
    block_index = jnp.arange(seq_count, dtype=jnp.int32)
    offset_index = jnp.arange(tokens, dtype=jnp.int32)
    cos_one, sin_one = angle_table(freq_one, block_index, 2 * seq_count)
    cos_inv, sin_inv = angle_table(block_index, freq_one, 2 * seq_count)
    cos_two, sin_two = angle_table(offset_index, offset_index, tokens)
    local_width = channels // seq_count
    arrived = (
        lax.all_to_all(mixed.T, "seq", split_axis=0, concat_axis=1, tiled=True),
        lax.all_to_all(gated.T, "seq", split_axis=0, concat_axis=1, tiled=True),
        lax.all_to_all(filter_taps.T, "seq", split_axis=0, concat_axis=1, tiled=True),
    )
    cos_tw, sin_tw = angle_table(freq_one, offset_index, full_length)
    spectra = []
    for line_data in arrived:
        lines = line_data.reshape(local_width, seq_count, tokens)
        real_part, imag_part = rotate("kn,cnm->ckm", cos_one, sin_one, -1.0, lines, None, True)
        real_part, imag_part = twist(cos_tw, sin_tw, -1.0, real_part, imag_part)
        spectra.append(rotate("jm,ckm->ckj", cos_two, sin_two, -1.0, real_part, imag_part, True))
    packed_real, packed_imag, corr_real, corr_imag = spectral_terms(
        spectra[0][0], spectra[0][1], spectra[1][0], spectra[1][1], spectra[2][0], spectra[2][1]
    )
    pr_mid, pi_mid = rotate("mj,ckj->ckm", cos_two, sin_two, 1.0, packed_real, packed_imag, True)
    pr_mid, pi_mid = twist(cos_tw, sin_tw, 1.0, pr_mid, pi_mid)
    cr_mid, ci_mid = rotate("mj,ckj->ckm", cos_two, sin_two, 1.0, corr_real, corr_imag, True)
    cr_mid, ci_mid = twist(cos_tw, sin_tw, 1.0, cr_mid, ci_mid)
    conv_lines, back_lines = rotate("nk,ckm->cnm", cos_inv, sin_inv, 1.0, pr_mid, pi_mid, True)
    corr_lines = rotate("nk,ckm->cnm", cos_inv, sin_inv, 1.0, cr_mid, ci_mid, False)[0]
    conv_lines = (conv_lines * inverse_scale).reshape(local_width, seq_length)
    back_lines = (back_lines * inverse_scale).reshape(local_width, seq_length)
    corr_lines = (corr_lines * inverse_scale).reshape(local_width, seq_length)
    returned = (
        lax.all_to_all(conv_lines, "seq", split_axis=1, concat_axis=0, tiled=True),
        lax.all_to_all(back_lines, "seq", split_axis=1, concat_axis=0, tiled=True),
        lax.all_to_all(corr_lines, "seq", split_axis=1, concat_axis=0, tiled=True),
    )
    conv_time = returned[0].T
    back_time = returned[1].T
    corr_time = returned[2].T
    conv_full = conv_time + skip_gain * mixed
    back_full = back_time + skip_gain * gated
    grad_query = (out_f * conv_full).astype(jnp.bfloat16)[None]
    grad_key = (back_full * value_f).astype(jnp.bfloat16)[None]
    grad_value = (back_full * key_f).astype(jnp.bfloat16)[None]
    grad_filter = lax.psum_scatter(
        corr_time * seq_length ** (-0.5), "ch", scatter_dimension=1, tiled=True
    )
    return (grad_query, grad_key, grad_value, grad_filter)


LANES = 128
VMEM_LIMIT = 60 * 1024 * 1024


def times_root(pair, turn, size):
    real, imag = pair
    turn %= size
    if turn == 0:
        return pair
    if 4 * turn == size:
        return (-imag, real)
    if 2 * turn == size:
        return (-real, -imag)
    if 4 * turn == 3 * size:
        return (imag, -real)
    cosine = math.cos(2.0 * math.pi * turn / size)
    sine = math.sin(2.0 * math.pi * turn / size)
    return (real * cosine - imag * sine, real * sine + imag * cosine)


def complex_dft(values, sense):
    size = len(values)
    if size == 1:
        return values
    even = complex_dft(values[0::2], sense)
    odd = complex_dft(values[1::2], sense)
    low, high = [], []
    for k in range(size // 2):
        er, ei = even[k]
        tr, ti = times_root(odd[k], sense * k, size)
        low.append((er + tr, ei + ti))
        high.append((er - tr, ei - ti))
    return low + high


def half_spectrum(values, size):
    if size == 2:
        return [(values[0] + values[1], None), (values[0] - values[1], None)]
    half, quarter = size // 2, size // 4
    if len(values) == half:
        total, difference = values, values
    else:
        total = [values[n] + values[n + half] for n in range(half)]
        difference = [values[n] - values[n + half] for n in range(half)]
    out = [None] * (half + 1)
    out[0::2] = half_spectrum(total, half)
    turned = [times_root((difference[n], -difference[n + quarter]), -n, size) for n in range(quarter)]
    for index, (real, imag) in enumerate(complex_dft(turned, -1)):
        k = 1 + 4 * index
        if k <= half:
            out[k] = (real, imag)
        else:
            out[size - k] = (real, -imag)
    return out


def real_from_half(terms, size, first_half):
    if size == 2:
        return [terms[0][0] + terms[1][0], terms[0][0] - terms[1][0]]
    half, quarter = size // 2, size // 4
    even = real_from_half(terms[0::2], half, False)
    chosen = []
    for index in range(quarter):
        k = 1 + 4 * index
        if k <= half:
            chosen.append(terms[k])
        else:
            real, imag = terms[size - k]
            chosen.append((real, -imag))
    turned = [times_root(pair, n, size) for n, pair in enumerate(complex_dft(chosen, 1))]
    odd = [pair[0] for pair in turned] + [-pair[1] for pair in turned]
    out = [even[n] + odd[n] for n in range(half)]
    if first_half:
        return out
    return out + [even[n] - odd[n] for n in range(half)]


def split_bf16(value):
    high = value.astype(jnp.bfloat16)
    return high, (value - high.astype(jnp.float32)).astype(jnp.bfloat16)


def three_dot(table_high, table_low, value):
    high, low = split_bf16(value)
    dot = lambda a, b: jnp.dot(a, b, preferred_element_type=jnp.float32)
    return dot(table_high, high) + (dot(table_high, low) + dot(table_low, high))


def far_first(seq_count, ch_count):
    steps = sorted(range(seq_count), key=lambda step: abs(2 * step - seq_count))
    return [(step, turn) for step in steps for turn in range(ch_count) if step or turn]


def partner_of(step, turn, seq_count, ch_count, me_seq, me_ch):
    return {"seq": lax.rem(me_seq + step, seq_count), "ch": lax.rem(me_ch + turn, ch_count)}


def left_mask(shape):
    return lax.broadcasted_iota(jnp.int32, shape, 1) < LANES // 2


def swap_halves(value):
    return pltpu.roll(value, LANES // 2, 1)


def greet_all(seq_count, ch_count, me_seq, me_ch):
    barrier = pltpu.get_barrier_semaphore()
    for step, turn in far_first(seq_count, ch_count):
        pl.semaphore_signal(barrier, inc=1, device_id=partner_of(step, turn, seq_count, ch_count, me_seq, me_ch), device_id_type=pl.DeviceIdType.MESH)
    return barrier


def exchange(sends, turn, seq_count, ch_count, me_seq, me_ch):
    copies = []
    for step, at in far_first(seq_count, ch_count):
        if at != turn:
            continue
        partner = partner_of(step, turn, seq_count, ch_count, me_seq, me_ch)
        for source, target, send_sem, recv_sem, per_seq in sends:
            if per_seq:
                give, take, slot = partner["seq"], me_seq, step
            else:
                give, take, slot = partner["ch"] * seq_count + partner["seq"], me_ch * seq_count + me_seq, step * ch_count + turn
            copy = pltpu.make_async_remote_copy(
                src_ref=source.at[give],
                dst_ref=target.at[take],
                send_sem=send_sem.at[slot],
                recv_sem=recv_sem.at[slot],
                device_id=partner,
                device_id_type=pl.DeviceIdType.MESH,
            )
            copy.start()
            copies.append(copy)
    return copies


def layer_kernel(
    seq_count, ch_count,
    query_ref, key_ref, value_ref, out_ref, filter_ref, skip_ref, fwd_ref, inv_ref, tw_ref,
    gq_ref, gk_ref, gv_ref, gf_ref,
    send, taps_send, recv, taps_recv, result, corr_result, back_recv, corr_recv,
    spec, taps_spec, corr_spec, taps_scr, corr_scr, tw_scr,
    send_sem, recv_sem, taps_send_sem, taps_recv_sem, back_send_sem, back_recv_sem, corr_send_sem, corr_recv_sem,
):
    me_seq, me_ch = lax.axis_index("seq"), lax.axis_index("ch")
    where_am_i = (seq_count, ch_count, me_seq, me_ch)
    tokens, channels = key_ref.shape
    half_tokens = tokens // 2
    size = 2 * seq_count
    scale = (seq_count * tokens) ** -0.5
    own = me_ch * (channels // ch_count)
    mine = me_ch * seq_count + me_seq
    barrier = greet_all(*where_am_i)

    def prepare_taps(group, carry):
        lanes = pl.ds(pl.multiple_of(own + group * LANES, LANES), LANES)
        taps = filter_ref[:, lanes].astype(jnp.float32) * scale
        top, bottom = taps[:half_tokens], taps[half_tokens:]
        left = left_mask(top.shape)
        taps_send[2 * group] = jnp.where(left, top, swap_halves(bottom))
        taps_send[2 * group + 1] = jnp.where(left, swap_halves(top), bottom)
        return carry

    lax.fori_loop(0, seq_count // 2, prepare_taps, 0)

    pl.semaphore_wait(barrier, len(far_first(seq_count, ch_count)))
    arriving = [exchange([(taps_send, taps_recv, taps_send_sem, taps_recv_sem, True)], 0, *where_am_i)]

    def prepare(group, carry):
        lanes = pl.ds(pl.multiple_of(group * LANES, LANES), LANES)
        mixed = key_ref[:, lanes].astype(jnp.float32) * value_ref[:, lanes].astype(jnp.float32)
        gated = out_ref[:, lanes].astype(jnp.float32) * query_ref[:, lanes].astype(jnp.float32)
        left = left_mask(mixed.shape)
        send[2 * group] = jnp.where(left, mixed, swap_halves(gated))
        send[2 * group + 1] = jnp.where(left, swap_halves(mixed), gated)
        return carry

    groups = seq_count // ch_count
    first_group = me_ch * groups
    other_group = lax.rem(me_ch + 1, ch_count) * groups
    lax.fori_loop(first_group, first_group + groups, prepare, 0)
    arriving[0] += exchange([(send, recv, send_sem, recv_sem, False)], 0, *where_am_i)
    lax.fori_loop(other_group, other_group + groups, prepare, 0)
    arriving.append(exchange([(send, recv, send_sem, recv_sem, False)], 1, *where_am_i))
    recv[mine] = send[mine]
    taps_recv[me_seq] = taps_send[me_seq]
    for k in range(seq_count + 1):
        for part in range(2):
            tw_scr[k, part] = jnp.broadcast_to(tw_ref[part, :, k:k + 1], (tokens, LANES))
    for copy in arriving[0]:
        copy.wait_recv()

    def spread_taps(block, carry):
        packed = taps_recv[block]
        rolled = swap_halves(packed)
        left = left_mask(packed.shape)
        taps_scr[block, :half_tokens, :] = jnp.where(left, packed, rolled)
        taps_scr[block, half_tokens:, :] = jnp.where(left, rolled, packed)
        return carry

    lax.fori_loop(0, seq_count, spread_taps, 0)

    def analyse(load, target):
        def body(chunk, carry):
            rows = pl.ds(pl.multiple_of(chunk * 8, 8), 8)
            for k, (real, imag) in enumerate(half_spectrum([load(n, rows) for n in range(seq_count)], size)):
                target[k, 0, rows, :] = real
                target[k, 1, rows, :] = jnp.zeros_like(real) if imag is None else imag
            return carry

        lax.fori_loop(0, tokens // 8, body, 0)

    def synthesise(source, store):
        def body(chunk, carry):
            rows = pl.ds(pl.multiple_of(chunk * 8, 8), 8)
            terms = [(source[k, 0, rows, :], source[k, 1, rows, :]) for k in range(seq_count + 1)]
            for n, value in enumerate(real_from_half(terms, size, True)):
                store(n, rows, value)
            return carry

        lax.fori_loop(0, tokens // 8, body, 0)

    def across(tables, real, imag):
        both = three_dot(tables[0], tables[1], jnp.concatenate([real, imag], axis=0))
        return both[:tokens], both[tokens:]

    def convolve(batch, first):
        base = batch * seq_count
        analyse(lambda n, rows: recv[base + n, rows, :], spec)
        if first:
            analyse(lambda n, rows: taps_scr[n, rows, :], taps_spec)
        forward = (fwd_ref[0], fwd_ref[1])
        inverse = (inv_ref[0], inv_ref[1])

        def middle(k, carry):
            cosine, sine = tw_scr[k, 0], tw_scr[k, 1]
            real, imag = spec[k, 0], spec[k, 1]
            real, imag = real * cosine + imag * sine, imag * cosine - real * sine
            if first:
                tr, ti = taps_spec[k, 0], taps_spec[k, 1]
                tr, ti = tr * cosine + ti * sine, ti * cosine - tr * sine
                real, imag = across(forward, jnp.concatenate([real, tr], axis=1), jnp.concatenate([imag, ti], axis=1))
                h_r, h_i = real[:, LANES:], imag[:, LANES:]
                a_r, a_i = real[:, :LANES], imag[:, :LANES]
                h_i = jnp.where(left_mask(h_i.shape), h_i, -h_i)
                taps_spec[k, 0], taps_spec[k, 1] = h_r, h_i
            else:
                a_r, a_i = across(forward, real, imag)
                h_r, h_i = taps_spec[k, 0], taps_spec[k, 1]
            g_r, g_i = swap_halves(a_r), swap_halves(a_i)
            c_r, c_i = a_r * g_r + a_i * g_i, a_r * g_i - a_i * g_r
            p_r, p_i = a_r * h_r - a_i * h_i, a_r * h_i + a_i * h_r
            weight = jnp.where((k == 0) | (k == seq_count), 0.5 / (seq_count * tokens), 1.0 / (seq_count * tokens))
            cosine, sine = cosine * weight, sine * weight
            if first:
                corr_spec[k, 0], corr_spec[k, 1] = c_r, c_i
                br, bi = across(inverse, p_r, p_i)
            else:
                c_r, c_i = c_r + corr_spec[k, 0], c_i + corr_spec[k, 1]
                both_r, both_i = across(inverse, jnp.concatenate([p_r, c_r], axis=1), jnp.concatenate([p_i, c_i], axis=1))
                br, bi = both_r[:, :LANES], both_i[:, :LANES]
                cr, ci = both_r[:, LANES:], both_i[:, LANES:]
                corr_spec[k, 0] = cr * cosine - ci * sine
                corr_spec[k, 1] = ci * cosine + cr * sine
            spec[k, 0] = br * cosine - bi * sine
            spec[k, 1] = bi * cosine + br * sine
            return carry

        lax.fori_loop(0, seq_count + 1, middle, 0)

        def store(n, rows, value):
            result[base + n, rows, :] = value

        synthesise(spec, store)

    returning = [(result, back_recv, back_send_sem, back_recv_sem, False)]
    convolve(me_ch, True)
    leaving = [exchange(returning, 0, *where_am_i)]
    for copy in arriving[1]:
        copy.wait_recv()
    convolve(lax.rem(me_ch + 1, ch_count), False)
    leaving.append(exchange(returning, 1, *where_am_i))

    def store_corr(n, rows, value):
        corr_scr[n, rows, :] = value

    synthesise(corr_spec, store_corr)

    def gather_corr(block, carry):
        top = corr_scr[block, :half_tokens, :]
        bottom = swap_halves(corr_scr[block, half_tokens:, :])
        corr_result[block] = jnp.where(left_mask(top.shape), top, bottom) * scale
        return carry

    lax.fori_loop(0, seq_count, gather_corr, 0)
    last = exchange([(corr_result, corr_recv, corr_send_sem, corr_recv_sem, True)], 0, *where_am_i)
    back_recv[mine] = result[mine]
    corr_recv[me_seq] = corr_result[me_seq]

    def finish(group, carry):
        lanes = pl.ds(pl.multiple_of(group * LANES, LANES), LANES)
        query_f = query_ref[:, lanes].astype(jnp.float32)
        key_f = key_ref[:, lanes].astype(jnp.float32)
        value_f = value_ref[:, lanes].astype(jnp.float32)
        out_f = out_ref[:, lanes].astype(jnp.float32)
        one, two = back_recv[2 * group], back_recv[2 * group + 1]
        left = left_mask(one.shape)
        skip = skip_ref[:, lanes]
        conv = jnp.where(left, one, swap_halves(two)) + skip * (key_f * value_f)
        back = jnp.where(left, swap_halves(one), two) + skip * (out_f * query_f)
        gq_ref[:, lanes] = (out_f * conv).astype(jnp.bfloat16)
        gk_ref[:, lanes] = (back * value_f).astype(jnp.bfloat16)
        gv_ref[:, lanes] = (back * key_f).astype(jnp.bfloat16)
        return carry

    for copy in leaving[0]:
        copy.wait_recv()
    lax.fori_loop(first_group, first_group + groups, finish, 0)
    for copy in leaving[1]:
        copy.wait_recv()
    lax.fori_loop(other_group, other_group + groups, finish, 0)
    for copy in last:
        copy.wait_recv()

    def finish_corr(group, carry):
        lanes = pl.ds(pl.multiple_of(group * LANES, LANES), LANES)
        one, two = corr_recv[2 * group], corr_recv[2 * group + 1]
        left = left_mask(one.shape)
        gf_ref[:half_tokens, lanes] = jnp.where(left, one, swap_halves(two))
        gf_ref[half_tokens:, lanes] = jnp.where(left, swap_halves(one), two)
        return carry

    lax.fori_loop(0, seq_count // 2, finish_corr, 0)
    for copy in arriving[0] + arriving[1] + leaving[0] + leaving[1] + last:
        copy.wait_send()


def tables(seq_count, tokens):
    index = np.arange(tokens)
    angle = 2.0 * np.pi / tokens * (index[:, None] * index[None, :] % tokens)
    cosine, sine = np.cos(angle), np.sin(angle)
    forward = np.block([[cosine, sine], [-sine, cosine]]).astype(np.float32)
    inverse = np.block([[cosine, -sine], [sine, cosine]]).astype(np.float32)

    def pieces(table):
        table = jnp.asarray(table)
        return jnp.stack(split_bf16(table))

    turn = 2.0 * np.pi / (2 * seq_count * tokens) * (np.arange(seq_count + 1)[:, None] * index[None, :])
    twiddle = jnp.asarray(np.stack([np.cos(turn).T, np.sin(turn).T]).astype(np.float32))
    return pieces(forward), pieces(inverse), twiddle


def fast_shards(query_gate, key_input, value_input, grad_output, filter_raw, skip_gain):
    seq_count, ch_count = lax.axis_size("seq"), lax.axis_size("ch")
    owners = seq_count * ch_count
    _, tokens, channels = key_input.shape
    vmem = pl.BlockSpec(memory_space=pltpu.VMEM)
    chunks = pltpu.VMEM((owners, tokens, LANES), jnp.float32)
    halves = pltpu.VMEM((seq_count, tokens // 2, LANES), jnp.float32)
    spectrum = pltpu.VMEM((seq_count + 1, 2, tokens, LANES), jnp.float32)
    lines = pltpu.VMEM((seq_count, tokens, LANES), jnp.float32)
    per_owner = pltpu.SemaphoreType.DMA((owners,))
    per_seq = pltpu.SemaphoreType.DMA((seq_count,))
    grads = pl.pallas_call(
        lambda *refs: layer_kernel(seq_count, ch_count, *refs),
        in_specs=[vmem] * 9,
        out_specs=[vmem] * 4,
        out_shape=[jax.ShapeDtypeStruct((tokens, channels), jnp.bfloat16)] * 3
        + [jax.ShapeDtypeStruct((tokens, channels // ch_count), jnp.float32)],
        scratch_shapes=[
            chunks, halves, chunks, halves, chunks, halves, chunks, halves,
            spectrum, spectrum, spectrum, lines, lines, spectrum,
            per_owner, per_owner, per_seq, per_seq, per_owner, per_owner, per_seq, per_seq,
        ],
        compiler_params=pltpu.CompilerParams(vmem_limit_bytes=VMEM_LIMIT, collective_id=0, has_side_effects=True),
        name="layer",
    )(query_gate[0], key_input[0], value_input[0], grad_output[0], filter_raw, skip_gain[None], *tables(seq_count, tokens))
    return (grads[0][None], grads[1][None], grads[2][None], grads[3])


def solution(mesh):
    in_specs = (
        P("ch", "seq", None),
        P("ch", "seq", None),
        P("ch", "seq", None),
        P("ch", "seq", None),
        P("seq", None),
        P(),
    )
    out_specs = (P("ch", "seq", None), P("ch", "seq", None), P("ch", "seq", None), P("seq", "ch"))

    def body(*arrays):
        seq_count, ch_count = mesh.shape["seq"], mesh.shape["ch"]
        _, tokens, channels = arrays[0].shape
        fits = ch_count == 2 and tokens == LANES and channels == seq_count * LANES and seq_count <= 32
        return (fast_shards if fits else shards)(*arrays)

    return jax.shard_map(body, mesh=mesh, in_specs=in_specs, out_specs=out_specs, check_vma=False)
```

profile of v0, /device:TPU:16, one launch (start us, length us, event | category | flops | bytes accessed | tf_op | source)
XLA Modules:
  0.0 130.1 jit_solution(4383641437918287933)
XLA Ops:
  0.6 124.3 %layer.1 = (bf16[128,2048]{1,0:T(8,128)(2,1)}, bf16[128,2048]{1,0:T(8,128)(2,1)}, bf16[128,2048]{1,0:T(8,128)(2,1)}, f32[128,1024]{1,0:T(8,128)}) custom-call(bf16[128,2048]{1,0:T(8,128)(2,1)} %bitcast.8, bf16[128,2048]{1,0:T(8,128)(2,1)} %bitcast.9, bf16[128,2048]{1,0:T(8,128)(2,1)} %bitcast.10, bf16[128,2048]{1,0:T(8,128)(2,1)} %bitcast.11, ...), custom_call_target="tpu_custom_call" | custom-call | tf_op jit(solution)/shard_map/layer/pallas_call | solution.py:483
  124.9 0.0 copy-start.2
  124.9 1.9 %copy.17 = bf16[1,128,2048]{2,1,0:T(8,128)(2,1)} copy(bf16[1,128,2048]{2,1,0:T(8,128)(2,1)} %bitcast.14) | data formatting | bytes 1048576
  126.9 0.0 copy-done.2
  126.9 0.0 copy-start.1
  126.9 0.8 copy.18
  127.7 0.4 copy-done.1
  128.1 0.0 copy-start
  128.1 0.8 copy.19
  128.9 0.4 copy-done
  129.3 0.8 copy.20
Async XLA Ops:
  124.9 2.0 %copy-start.2 = (bf16[128,2048]{1,0:T(8,128)(2,1)S(1)}, bf16[128,2048]{1,0:T(8,128)(2,1)}, u32[]{:S(2)}) copy-start(bf16[128,2048]{1,0:T(8,128)(2,1)} %get-tuple-element.9) | copy-start | bytes 1572868
  126.9 1.2 copy-start.1
  128.1 1.2 copy-start
where the time goes:
time: 131 us; the launch traced here: 130 us
  Pallas kernels  124 us (95%)
  local copies, waits for them, and re-layouts  5.19 us (4%)
    pallas_call x1, Pallas kernels, fast_shards(): pl.pallas_call(lambda *refs: layer_kernel(seq_count, ch_count, *refs), in...  124 us
    unnamed x10, local copies, waits for them, and re-layouts  5.19 us

commit v1 on v0

v1 whole, which is shorter than its diff:
```python
import math

import numpy as np

import jax
import jax.numpy as jnp
from jax import lax
from jax.experimental import pallas as pl
from jax.experimental.pallas import tpu as pltpu
from jax.sharding import PartitionSpec as P


def angle_table(row_index, col_index, modulus):
    turn_count = row_index[:, None] * col_index[None, :] % modulus
    angles = turn_count.astype(jnp.float32) * (2.0 * math.pi / modulus)
    return (jnp.cos(angles), jnp.sin(angles))


def contract(pattern, table, operand):
    return jnp.einsum(
        pattern, table, operand, precision=lax.Precision.HIGHEST, preferred_element_type=jnp.float32
    )


def rotate(pattern, cos_table, sin_table, sense_sign, real_part, imag_part, want_imag):
    if imag_part is None:
        cos_term = contract(pattern, cos_table, real_part)
        return (cos_term, sense_sign * contract(pattern, sin_table, real_part))
    real_out = contract(pattern, cos_table, real_part) - sense_sign * contract(
        pattern, sin_table, imag_part
    )
    if not want_imag:
        return (real_out, None)
    imag_out = contract(pattern, cos_table, imag_part) + sense_sign * contract(
        pattern, sin_table, real_part
    )
    return (real_out, imag_out)


def twist(cos_table, sin_table, sense_sign, real_part, imag_part):
    return (
        real_part * cos_table - sense_sign * imag_part * sin_table,
        imag_part * cos_table + sense_sign * real_part * sin_table,
    )


def spectral_terms(z_real, z_imag, g_real, g_imag, h_real, h_imag):
    conv_real = z_real * h_real - z_imag * h_imag
    conv_imag = z_real * h_imag + z_imag * h_real
    back_real = h_real * g_real + h_imag * g_imag
    back_imag = h_real * g_imag - h_imag * g_real
    corr_real = z_real * g_real + z_imag * g_imag
    corr_imag = z_real * g_imag - z_imag * g_real
    return (conv_real - back_imag, conv_imag + back_real, corr_real, corr_imag)


def shards(query_gate, key_input, value_input, grad_output, filter_raw, skip_gain):
    seq_count = lax.axis_size("seq")
    key_f = key_input[0].astype(jnp.float32)
    value_f = value_input[0].astype(jnp.float32)
    out_f = grad_output[0].astype(jnp.float32)
    mixed = key_f * value_f
    gated = out_f * query_gate[0].astype(jnp.float32)
    tokens, channels = mixed.shape
    seq_length = tokens * seq_count
    full_length = 2 * seq_length
    inverse_scale = 1.0 / full_length
    filter_taps = filter_raw.astype(jnp.float32) * seq_length ** (-0.5)
    freq_one = jnp.arange(2 * seq_count, dtype=jnp.int32)
    block_index = jnp.arange(seq_count, dtype=jnp.int32)
    offset_index = jnp.arange(tokens, dtype=jnp.int32)
    cos_one, sin_one = angle_table(freq_one, block_index, 2 * seq_count)
    cos_inv, sin_inv = angle_table(block_index, freq_one, 2 * seq_count)
    cos_two, sin_two = angle_table(offset_index, offset_index, tokens)
    local_width = channels // seq_count
    arrived = (
        lax.all_to_all(mixed.T, "seq", split_axis=0, concat_axis=1, tiled=True),
        lax.all_to_all(gated.T, "seq", split_axis=0, concat_axis=1, tiled=True),
        lax.all_to_all(filter_taps.T, "seq", split_axis=0, concat_axis=1, tiled=True),
    )
    cos_tw, sin_tw = angle_table(freq_one, offset_index, full_length)
    spectra = []
    for line_data in arrived:
        lines = line_data.reshape(local_width, seq_count, tokens)
        real_part, imag_part = rotate("kn,cnm->ckm", cos_one, sin_one, -1.0, lines, None, True)
        real_part, imag_part = twist(cos_tw, sin_tw, -1.0, real_part, imag_part)
        spectra.append(rotate("jm,ckm->ckj", cos_two, sin_two, -1.0, real_part, imag_part, True))
    packed_real, packed_imag, corr_real, corr_imag = spectral_terms(
        spectra[0][0], spectra[0][1], spectra[1][0], spectra[1][1], spectra[2][0], spectra[2][1]
    )
    pr_mid, pi_mid = rotate("mj,ckj->ckm", cos_two, sin_two, 1.0, packed_real, packed_imag, True)
    pr_mid, pi_mid = twist(cos_tw, sin_tw, 1.0, pr_mid, pi_mid)
    cr_mid, ci_mid = rotate("mj,ckj->ckm", cos_two, sin_two, 1.0, corr_real, corr_imag, True)
    cr_mid, ci_mid = twist(cos_tw, sin_tw, 1.0, cr_mid, ci_mid)
    conv_lines, back_lines = rotate("nk,ckm->cnm", cos_inv, sin_inv, 1.0, pr_mid, pi_mid, True)
    corr_lines = rotate("nk,ckm->cnm", cos_inv, sin_inv, 1.0, cr_mid, ci_mid, False)[0]
    conv_lines = (conv_lines * inverse_scale).reshape(local_width, seq_length)
    back_lines = (back_lines * inverse_scale).reshape(local_width, seq_length)
    corr_lines = (corr_lines * inverse_scale).reshape(local_width, seq_length)
    returned = (
        lax.all_to_all(conv_lines, "seq", split_axis=1, concat_axis=0, tiled=True),
        lax.all_to_all(back_lines, "seq", split_axis=1, concat_axis=0, tiled=True),
        lax.all_to_all(corr_lines, "seq", split_axis=1, concat_axis=0, tiled=True),
    )
    conv_time = returned[0].T
    back_time = returned[1].T
    corr_time = returned[2].T
    conv_full = conv_time + skip_gain * mixed
    back_full = back_time + skip_gain * gated
    grad_query = (out_f * conv_full).astype(jnp.bfloat16)[None]
    grad_key = (back_full * value_f).astype(jnp.bfloat16)[None]
    grad_value = (back_full * key_f).astype(jnp.bfloat16)[None]
    grad_filter = lax.psum_scatter(
        corr_time * seq_length ** (-0.5), "ch", scatter_dimension=1, tiled=True
    )
    return (grad_query, grad_key, grad_value, grad_filter)


LANES = 128
VMEM_LIMIT = 60 * 1024 * 1024


def times_root(pair, turn, size):
    real, imag = pair
    turn %= size
    if turn == 0:
        return pair
    if 4 * turn == size:
        return (-imag, real)
    if 2 * turn == size:
        return (-real, -imag)
    if 4 * turn == 3 * size:
        return (imag, -real)
    cosine = math.cos(2.0 * math.pi * turn / size)
    sine = math.sin(2.0 * math.pi * turn / size)
    return (real * cosine - imag * sine, real * sine + imag * cosine)


def complex_dft(values, sense):
    size = len(values)
    if size == 1:
        return values
    even = complex_dft(values[0::2], sense)
    odd = complex_dft(values[1::2], sense)
    low, high = [], []
    for k in range(size // 2):
        er, ei = even[k]
        tr, ti = times_root(odd[k], sense * k, size)
        low.append((er + tr, ei + ti))
        high.append((er - tr, ei - ti))
    return low + high


def half_spectrum(values, size):
    if size == 2:
        return [(values[0] + values[1], None), (values[0] - values[1], None)]
    half, quarter = size // 2, size // 4
    if len(values) == half:
        total, difference = values, values
    else:
        total = [values[n] + values[n + half] for n in range(half)]
        difference = [values[n] - values[n + half] for n in range(half)]
    out = [None] * (half + 1)
    out[0::2] = half_spectrum(total, half)
    turned = [times_root((difference[n], -difference[n + quarter]), -n, size) for n in range(quarter)]
    for index, (real, imag) in enumerate(complex_dft(turned, -1)):
        k = 1 + 4 * index
        if k <= half:
            out[k] = (real, imag)
        else:
            out[size - k] = (real, -imag)
    return out


def real_from_half(terms, size, first_half):
    if size == 2:
        return [terms[0][0] + terms[1][0], terms[0][0] - terms[1][0]]
    half, quarter = size // 2, size // 4
    even = real_from_half(terms[0::2], half, False)
    chosen = []
    for index in range(quarter):
        k = 1 + 4 * index
        if k <= half:
            chosen.append(terms[k])
        else:
            real, imag = terms[size - k]
            chosen.append((real, -imag))
    turned = [times_root(pair, n, size) for n, pair in enumerate(complex_dft(chosen, 1))]
    odd = [pair[0] for pair in turned] + [-pair[1] for pair in turned]
    out = [even[n] + odd[n] for n in range(half)]
    if first_half:
        return out
    return out + [even[n] - odd[n] for n in range(half)]


def split_bf16(value):
    high = value.astype(jnp.bfloat16)
    return high, (value - high.astype(jnp.float32)).astype(jnp.bfloat16)


def three_dot(table_high, table_low, value):
    high, low = split_bf16(value)
    dot = lambda a, b: jnp.dot(a, b, preferred_element_type=jnp.float32)
    return dot(table_high, high) + (dot(table_high, low) + dot(table_low, high))


QUARTERS = 4
QUARTER = LANES // QUARTERS
PLAN = ((0, 1), (0, 2), (0, 3), (1, 1), (1, 2), (1, 3), (2, 1), (2, 2))
PLANES = 4
PLAN_STEP = 3
JOB_SLOTS = 3
LOCAL_SLOTS = 5


def left_mask(shape):
    return lax.broadcasted_iota(jnp.int32, shape, 1) < LANES // 2


def even_mask(shape):
    return lax.broadcasted_iota(jnp.int32, shape, 1) & QUARTER == 0


def swap_halves(value):
    return pltpu.roll(value, LANES // 2, 1)


def turn_quarters(value, count):
    count %= QUARTERS
    return pltpu.roll(value, count * QUARTER, 1) if count else value


def choose_quarters(values):
    lane = lax.broadcasted_iota(jnp.int32, values[0].shape, 1)
    out = values[-1]
    for index in reversed(range(QUARTERS - 1)):
        out = jnp.where(lane < (index + 1) * QUARTER, values[index], out)
    return out


def transpose_quarters(values):
    turned = [turn_quarters(value, index) for index, value in enumerate(values)]
    mixed = [choose_quarters([turned[(u - a) % QUARTERS] for u in range(QUARTERS)]) for a in range(QUARTERS)]
    return [turn_quarters(value, -index) for index, value in enumerate(mixed)]


def interleave(one, two):
    even = even_mask(one.shape)
    return jnp.where(even, one, turn_quarters(two, 1)), jnp.where(even, turn_quarters(one, -1), two)


def offsets(count):
    return sorted(range(count), key=lambda step: abs(2 * step - count))


def greet_all(seq_count, ch_count, me_seq, me_ch):
    barrier = pltpu.get_barrier_semaphore()
    for step in offsets(seq_count):
        for turn in range(ch_count):
            if step or turn:
                partner = {"seq": lax.rem(me_seq + step, seq_count), "ch": lax.rem(me_ch + turn, ch_count)}
                pl.semaphore_signal(barrier, inc=1, device_id=partner, device_id_type=pl.DeviceIdType.MESH)
    return barrier


def layer_kernel(
    seq_count, ch_count,
    query_ref, key_ref, value_ref, out_ref, filter_ref, skip_ref, fwd_ref, inv_ref, tw_ref,
    gq_ref, gk_ref, gv_ref, gf_ref,
    send, send_half, taps_send, recv, recv_half, taps_recv,
    result, result_half, corr_result, back, back_half, corr, corr_far,
    lines, taps_lines, spec, taps_spec, corr_spec, tw_scr,
    send_sem, half_send_sem, taps_send_sem, local_taps_send_sem,
    recv_sem, half_recv_sem, taps_recv_sem,
    back_send_sem, back_half_send_sem, corr_send_sem,
    back_sem, back_half_sem, corr_sem, corr_far_sem,
):
    me_seq, me_ch = lax.axis_index("seq"), lax.axis_index("ch")
    tokens, channels = key_ref.shape
    half_tokens, part_tokens = tokens // 2, tokens // QUARTERS
    half_seq = seq_count // 2
    width = seq_count // PLANES
    plane, place = lax.div(me_seq, width), lax.rem(me_seq, width)
    high = lax.div(plane, PLANES // 2)
    low = 1 - high
    scale = (seq_count * tokens) ** -0.5
    side_channels = channels // ch_count
    jobs = QUARTERS * len(PLAN)
    far_groups = [group for group, (_, owner) in enumerate(PLAN) if owner >= PLANES // 2]
    far_jobs = QUARTERS * len(far_groups)
    own = [[group for group, (at, owner) in enumerate(PLAN) if owner == p] for p in range(PLANES)]
    own[0] = far_groups
    kept = [len(groups) for groups in own]
    barrier = greet_all(seq_count, ch_count, me_seq, me_ch)

    def start(source, target, seq, ch, send_at, recv_at):
        pltpu.make_async_remote_copy(
            src_ref=source, dst_ref=target, send_sem=send_at, recv_sem=recv_at,
            device_id={"seq": seq, "ch": ch}, device_id_type=pl.DeviceIdType.MESH,
        ).start()

    def span(ref, count, send_at, recv_at):
        return pltpu.make_async_remote_copy(
            src_ref=ref.at[pl.ds(0, count)], dst_ref=ref.at[pl.ds(0, count)], send_sem=send_at, recv_sem=recv_at,
            device_id={"seq": me_seq, "ch": me_ch}, device_id_type=pl.DeviceIdType.MESH,
        )

    def arrive(ref, count, sem):
        span(ref, count, sem, sem).wait_recv()

    def depart(ref, count, sem):
        if count:
            span(ref, count, sem, sem).wait_send()

    def prepare(group, side):
        lanes = pl.ds(pl.multiple_of(side * side_channels + group * LANES, LANES), LANES)
        base = side * jobs + QUARTERS * group

        def body(chunk, carry):
            pieces = []
            rows = [pl.ds(pl.multiple_of(chunk * 16 + first, 16), 16) for first in (0, half_tokens)]
            for one, two in ((key_ref, value_ref), (out_ref, query_ref)):
                for at in rows:
                    pieces.append(one[at, lanes].astype(jnp.float32) * two[at, lanes].astype(jnp.float32))
            for index, piece in enumerate(transpose_quarters(pieces)):
                send[base + index, rows[0], :] = piece
            return carry

        lax.fori_loop(0, half_tokens // 16, body, 0)

    def halve(group, side):
        far = group - 1 - lax.div(group, PLAN_STEP)
        for index in range(QUARTERS):
            piece = send[side * jobs + QUARTERS * group + index]
            top, bottom = piece[:part_tokens], piece[part_tokens:]
            send_half[side * far_jobs + QUARTERS * far + index] = jnp.where(left_mask(top.shape), top, swap_halves(bottom))

    def prepare_taps(group):
        lanes = pl.ds(pl.multiple_of(me_ch * side_channels + group * LANES, LANES), LANES)
        pieces = [filter_ref[part_tokens * k:part_tokens * (k + 1), lanes].astype(jnp.float32) * scale for k in range(QUARTERS)]
        for index, piece in enumerate(transpose_quarters(pieces)):
            taps_send[QUARTERS * group + index] = piece

    def turns():
        return [(step, turn) for step in offsets(width) for turn in reversed(range(ch_count))]

    def send_taps(group):
        slot = lax.div(group, PLAN_STEP)
        owner = 1 + lax.rem(group, PLAN_STEP)
        far = group - 1 - slot
        is_far = owner > 1
        for step in offsets(width):
            at = lax.rem(place + step, width)
            source = taps_send.at[QUARTERS * group + at]

            def to_owner():
                start(source, taps_recv.at[slot * seq_count + me_seq], owner * width + at, me_ch, taps_send_sem, taps_recv_sem.at[slot])

            def to_local():
                start(source, taps_recv.at[far * half_seq + me_seq], at, me_ch, local_taps_send_sem, taps_recv_sem.at[far])

            if step:
                to_owner()
                pl.when(is_far & (low == 1))(to_local)
            else:
                pl.when(plane != owner)(to_owner)

                @pl.when(plane == owner)
                def _():
                    taps_recv[slot * seq_count + me_seq] = taps_send[QUARTERS * group + place]

                pl.when(is_far & (low == 1) & (plane != 0))(to_local)

                @pl.when(is_far & (plane == 0))
                def _():
                    taps_recv[far * half_seq + me_seq] = taps_send[QUARTERS * group + place]

    def send_group(group):
        slot = lax.div(group, PLAN_STEP)
        owner = 1 + lax.rem(group, PLAN_STEP)
        far = group - 1 - slot

        @pl.when((owner > 1) & (low == 1))
        def _():
            for step, turn in turns():
                at, ch = lax.rem(place + step, width), lax.rem(me_ch + turn, ch_count)
                start(
                    send_half.at[ch * far_jobs + QUARTERS * far + at],
                    recv_half.at[slot * seq_count + me_ch * half_seq + me_seq],
                    owner * width + at, ch, half_send_sem, half_recv_sem.at[slot],
                )

        def whole(target_plane, target_slot, index):
            for step, turn in turns():
                at, ch = lax.rem(place + step, width), lax.rem(me_ch + turn, ch_count)

                def go():
                    start(send.at[ch * jobs + QUARTERS * group + at], recv.at[index], target_plane * width + at, ch, send_sem, recv_sem.at[target_slot])

                if step or turn:
                    go()
                else:
                    pl.when(plane != target_plane)(go)

                    @pl.when(plane == target_plane)
                    def _():
                        recv[index] = send[me_ch * jobs + QUARTERS * group + place]

        @pl.when((owner == 1) | (high == 1))
        def _():
            whole(owner, slot, (slot * ch_count + me_ch) * seq_count + me_seq)

        @pl.when((owner > 1) & (low == 1))
        def _():
            whole(0, far, (far * ch_count + me_ch) * half_seq + me_seq)

    def ready(group):
        other = lax.rem(me_ch + 1, ch_count)
        prepare_taps(group)
        prepare(group, other)
        prepare(group, me_ch)
        slot = lax.div(group, PLAN_STEP)

        @pl.when((group - PLAN_STEP * slot > 0) & (low == 1))
        def _():
            halve(group, 0)
            halve(group, 1)

    ready(0)
    pl.semaphore_wait(barrier, seq_count * ch_count - 1)

    def feed(group, carry):
        pl.when(group > 0)(lambda: ready(group))
        send_group(group)
        send_taps(group)
        return carry

    lax.fori_loop(0, len(PLAN), feed, 0)
    for k in range(seq_count + 1):
        for part in range(2):
            tw_scr[k, part] = jnp.broadcast_to(tw_ref[part, :, k:k + 1], (tokens, LANES))

    def analyse(source, target, blocks):
        def body(chunk, carry):
            rows = pl.ds(pl.multiple_of(chunk * 8, 8), 8)
            for k, (real, imag) in enumerate(half_spectrum([source[n, rows, :] for n in range(blocks)], 2 * blocks)):
                target[k, 0, rows, :] = real
                target[k, 1, rows, :] = jnp.zeros_like(real) if imag is None else imag
            return carry

        lax.fori_loop(0, tokens // 8, body, 0)

    def synthesise(source, target, blocks):
        def body(chunk, carry):
            rows = pl.ds(pl.multiple_of(chunk * 8, 8), 8)
            terms = [(source[k, 0, rows, :], source[k, 1, rows, :]) for k in range(blocks + 1)]
            for n, value in enumerate(real_from_half(terms, 2 * blocks, True)):
                target[n, rows, :] = value
            return carry

        lax.fori_loop(0, tokens // 8, body, 0)

    def across(table, real, imag):
        both = three_dot(table[0], table[1], jnp.concatenate([real, imag], axis=0))
        return both[:tokens], both[tokens:]

    def convolve(blocks):
        stride = seq_count // blocks
        analyse(lines, spec, blocks)
        analyse(taps_lines, taps_spec, blocks)
        forward = (fwd_ref[0], fwd_ref[1])
        inverse = (inv_ref[0], inv_ref[1])

        def middle(k, carry):
            cosine, sine = tw_scr[stride * k, 0], tw_scr[stride * k, 1]
            real, imag = spec[k, 0], spec[k, 1]
            real, imag = real * cosine + imag * sine, imag * cosine - real * sine
            tr, ti = taps_spec[k, 0], taps_spec[k, 1]
            tr, ti = tr * cosine + ti * sine, ti * cosine - tr * sine
            real, imag = across(forward, jnp.concatenate([real, tr], axis=1), jnp.concatenate([imag, ti], axis=1))
            h_r, h_i = real[:, LANES:], imag[:, LANES:]
            a_r, a_i = real[:, :LANES], imag[:, :LANES]
            h_i = jnp.where(left_mask(h_i.shape), h_i, -h_i)
            g_r, g_i = swap_halves(a_r), swap_halves(a_i)
            c_r, c_i = a_r * g_r + a_i * g_i, a_r * g_i - a_i * g_r
            p_r, p_i = a_r * h_r - a_i * h_i, a_r * h_i + a_i * h_r
            weight = jnp.where((k == 0) | (k == blocks), 0.5 / (blocks * tokens), 1.0 / (blocks * tokens))
            cosine, sine = cosine * weight, sine * weight
            both_r, both_i = across(inverse, jnp.concatenate([p_r, c_r], axis=1), jnp.concatenate([p_i, c_i], axis=1))
            br, bi = both_r[:, :LANES], both_i[:, :LANES]
            cr, ci = both_r[:, LANES:], both_i[:, LANES:]
            spec[k, 0] = br * cosine - bi * sine
            spec[k, 1] = bi * cosine + br * sine
            corr_spec[k, 0] = cr * cosine - ci * sine
            corr_spec[k, 1] = ci * cosine + cr * sine
            return carry

        lax.fori_loop(0, blocks + 1, middle, 0)
        synthesise(spec, lines, blocks)
        synthesise(corr_spec, taps_lines, blocks)

    def open_taps(slot, blocks):
        def body(n, carry):
            packed = taps_recv[slot * blocks + n]
            turned = [turn_quarters(packed, count) for count in range(QUARTERS)]
            for k in range(QUARTERS):
                taps_lines[n, part_tokens * k:part_tokens * (k + 1), :] = choose_quarters([turned[(u - k) % QUARTERS] for u in range(QUARTERS)])
            return carry

        lax.fori_loop(0, blocks, body, 0)

    def open_whole(slot, blocks, first):
        def body(n, carry):
            base = slot * ch_count * blocks + n
            top, bottom = interleave(recv[base], recv[base + blocks])
            lines[n, :half_tokens, :] = top
            lines[n, half_tokens:, :] = bottom
            return carry

        lax.fori_loop(first, blocks, body, 0)

    def open_half(slot):
        def body(n, carry):
            one, two = recv_half[slot * seq_count + n], recv_half[slot * seq_count + half_seq + n]
            left = left_mask(one.shape)
            for first in (0, part_tokens):
                top, bottom = interleave(one, two)
                lines[n, first:first + part_tokens, :] = jnp.where(left, top, 0.0)
                lines[n, half_tokens + first:half_tokens + first + part_tokens, :] = jnp.where(left, bottom, 0.0)
                one, two = swap_halves(one), swap_halves(two)
            return carry

        lax.fori_loop(0, half_seq, body, 0)

    def close_whole(slot, blocks, first):
        def body(n, carry):
            base = slot * ch_count * blocks + n
            one, two = interleave(lines[n, :half_tokens, :], lines[n, half_tokens:, :])
            result[base] = one
            result[base + blocks] = two
            return carry

        lax.fori_loop(first, blocks, body, 0)

    def close_half(slot):
        def body(n, carry):
            for index, piece in enumerate(interleave(lines[n, :half_tokens, :], lines[n, half_tokens:, :])):
                top, bottom = piece[:part_tokens], piece[part_tokens:]
                result_half[slot * seq_count + index * half_seq + n] = jnp.where(left_mask(top.shape), swap_halves(bottom), top)
            return carry

        lax.fori_loop(0, half_seq, body, 0)

    def close_corr(slot, blocks):
        def body(n, carry):
            pieces = []
            for k in range(QUARTERS):
                piece = taps_lines[n, part_tokens * k:part_tokens * (k + 1), :]
                pieces.append(turn_quarters((piece + turn_quarters(piece, -1)) * scale, k))
            corr_result[slot * blocks + n] = choose_quarters(pieces)
            return carry

        lax.fori_loop(0, blocks, body, 0)

    def deliver(slot, blocks, group, first, count):
        job = QUARTERS * group + place
        at_round = lax.div(group, PLAN_STEP)
        base = slot * ch_count * blocks
        for step in offsets(count):
            seq = first + lax.rem(me_seq + step, count)
            for turn in range(ch_count):
                ch = lax.rem(me_ch + turn, ch_count)
                if step or turn:
                    start(result.at[base + ch * blocks + seq], back.at[me_ch * jobs + job], seq, ch, back_send_sem, back_sem.at[at_round])
            if step:
                start(corr_result.at[slot * blocks + seq], corr.at[job], seq, me_ch, corr_send_sem, corr_sem.at[at_round])
        back[me_ch * jobs + job] = result[base + me_ch * blocks + me_seq]
        corr[job] = corr_result[slot * blocks + me_seq]

    def deliver_half(slot, group):
        far = QUARTERS * (group - 1 - slot) + place
        for step in offsets(half_seq):
            seq = lax.rem(me_seq + step, half_seq)
            for turn in range(ch_count):
                ch = lax.rem(me_ch + turn, ch_count)
                start(
                    result_half.at[slot * seq_count + ch * half_seq + seq], back_half.at[me_ch * far_jobs + far],
                    seq, ch, back_half_send_sem, back_half_sem.at[slot],
                )
            start(corr_result.at[slot * seq_count + seq], corr_far.at[far], seq, me_ch, corr_send_sem, corr_far_sem.at[slot])

    others = seq_count * ch_count - 1

    def owner_job(slot, carry):
        group = PLAN_STEP * slot + plane - 1
        arrive(taps_recv, seq_count - 1, taps_recv_sem.at[slot])
        open_taps(slot, seq_count)

        @pl.when(high == 0)
        def _():
            arrive(recv, others, recv_sem.at[slot])
            open_whole(slot, seq_count, 0)

        @pl.when(high == 1)
        def _():
            arrive(recv_half, seq_count, half_recv_sem.at[slot])
            open_half(slot)
            arrive(recv, seq_count - 1, recv_sem.at[slot])
            open_whole(slot, seq_count, half_seq)

        convolve(seq_count)
        close_corr(slot, seq_count)

        @pl.when(high == 0)
        def _():
            close_whole(slot, seq_count, 0)
            deliver(slot, seq_count, group, 0, seq_count)

        @pl.when(high == 1)
        def _():
            close_half(slot)
            close_whole(slot, seq_count, half_seq)
            deliver_half(slot, group)
            deliver(slot, seq_count, group, half_seq, half_seq)

        return carry

    def local_job(slot, carry):
        group = slot + 1 + lax.div(slot, 2)
        arrive(taps_recv, half_seq - 1, taps_recv_sem.at[slot])
        open_taps(slot, half_seq)
        arrive(recv, seq_count - 1, recv_sem.at[slot])
        open_whole(slot, half_seq, 0)
        convolve(half_seq)
        close_corr(slot, half_seq)
        close_whole(slot, half_seq, 0)
        deliver(slot, half_seq, group, 0, half_seq)
        return carry

    @pl.when(plane > 0)
    def _():
        lax.fori_loop(0, JOB_SLOTS - lax.div(plane, PLANES - 1), owner_job, 0)

    @pl.when(plane == 0)
    def _():
        lax.fori_loop(0, LOCAL_SLOTS, local_job, 0)

    def finish(group, side):
        lanes = pl.ds(pl.multiple_of(side * side_channels + group * LANES, LANES), LANES)
        base = side * jobs + QUARTERS * group
        skip = skip_ref[:, lanes]

        def body(chunk, carry):
            rows = [pl.ds(pl.multiple_of(chunk * 16 + first, 16), 16) for first in (0, half_tokens)]
            pieces = transpose_quarters([back[base + index, rows[0], :] for index in range(QUARTERS)])
            for at, conv, behind in zip(rows, pieces[:2], pieces[2:]):
                query_f = query_ref[at, lanes].astype(jnp.float32)
                key_f = key_ref[at, lanes].astype(jnp.float32)
                value_f = value_ref[at, lanes].astype(jnp.float32)
                out_f = out_ref[at, lanes].astype(jnp.float32)
                conv = conv + skip * (key_f * value_f)
                behind = behind + skip * (out_f * query_f)
                gq_ref[at, lanes] = (out_f * conv).astype(jnp.bfloat16)
                gk_ref[at, lanes] = (behind * value_f).astype(jnp.bfloat16)
                gv_ref[at, lanes] = (behind * key_f).astype(jnp.bfloat16)
            return carry

        lax.fori_loop(0, half_tokens // 16, body, 0)

    def finish_corr(group):
        lanes = pl.ds(pl.multiple_of(group * LANES, LANES), LANES)
        pieces = transpose_quarters([corr[QUARTERS * group + index] for index in range(QUARTERS)])
        for k, piece in enumerate(pieces):
            gf_ref[part_tokens * k:part_tokens * (k + 1), lanes] = piece

    def join_half(far, group):
        for side in range(ch_count):
            for index in range(QUARTERS):
                piece = back_half[side * far_jobs + QUARTERS * far + index]
                left = left_mask(piece.shape)
                place_at = side * jobs + QUARTERS * group + index
                back[place_at, :part_tokens, :] += jnp.where(left, 0.0, piece)
                back[place_at, part_tokens:, :] += jnp.where(left, 0.0, swap_halves(piece))
        for index in range(QUARTERS):
            corr[QUARTERS * group + index] += corr_far[QUARTERS * far + index]

    for at_round in range(JOB_SLOTS):
        groups = [group for group, (when, _) in enumerate(PLAN) if when == at_round]
        for p in range(PLANES):
            mine = sum(PLAN[group][0] == at_round for group in own[p])

            @pl.when(plane == p)
            def _():
                arrive(back, QUARTERS * ch_count * len(groups) - mine, back_sem.at[at_round])
                arrive(corr, QUARTERS * len(groups) - mine, corr_sem.at[at_round])

        @pl.when(low == 1)
        def _():
            count = QUARTERS * sum(group in far_groups for group in groups)
            arrive(back_half, count * ch_count, back_half_sem.at[at_round])
            arrive(corr_far, count, corr_far_sem.at[at_round])
            for group in groups:
                if group in far_groups:
                    join_half(far_groups.index(group), group)

        def finish_group(index, carry):
            group = groups[0] + index
            finish(group, 0)
            finish(group, 1)
            finish_corr(group)
            return carry

        lax.fori_loop(0, len(groups), finish_group, 0)

    for p in range(PLANES):
        is_low = p < PLANES // 2
        count = kept[p]

        @pl.when(plane == p)
        def _():
            depart(send, ch_count * jobs - count, send_sem)
            depart(send_half, ch_count * far_jobs if is_low else 0, half_send_sem)
            depart(taps_send, jobs - (count if p else 0), taps_send_sem)
            depart(taps_send, far_jobs - (0 if p else count) if is_low else 0, local_taps_send_sem)
            whole = (others if is_low else seq_count - 1) if p else seq_count - 1
            depart(result, count * whole, back_send_sem)
            depart(result_half, 0 if is_low else count * seq_count, back_half_send_sem)
            depart(corr_result, count * ((seq_count if p else half_seq) - 1), corr_send_sem)


def tables(seq_count, tokens):
    index = np.arange(tokens)
    angle = 2.0 * np.pi / tokens * (index[:, None] * index[None, :] % tokens)
    cosine, sine = np.cos(angle), np.sin(angle)
    forward = np.block([[cosine, sine], [-sine, cosine]]).astype(np.float32)
    inverse = np.block([[cosine, -sine], [sine, cosine]]).astype(np.float32)

    def pieces(table):
        table = jnp.asarray(table)
        return jnp.stack(split_bf16(table))

    turn = 2.0 * np.pi / (2 * seq_count * tokens) * (np.arange(seq_count + 1)[:, None] * index[None, :])
    twiddle = jnp.asarray(np.stack([np.cos(turn).T, np.sin(turn).T]).astype(np.float32))
    return pieces(forward), pieces(inverse), twiddle


def fast_shards(query_gate, key_input, value_input, grad_output, filter_raw, skip_gain):
    seq_count, ch_count = lax.axis_size("seq"), lax.axis_size("ch")
    _, tokens, channels = key_input.shape
    vmem = pl.BlockSpec(memory_space=pltpu.VMEM)
    jobs = QUARTERS * len(PLAN)
    far_jobs = QUARTERS * LOCAL_SLOTS
    whole = lambda count: pltpu.VMEM((count, tokens // 2, LANES), jnp.float32)
    part = lambda count: pltpu.VMEM((count, tokens // QUARTERS, LANES), jnp.float32)
    spectrum = pltpu.VMEM((seq_count + 1, 2, tokens, LANES), jnp.float32)
    lines = pltpu.VMEM((seq_count, tokens, LANES), jnp.float32)
    slots = JOB_SLOTS * seq_count
    single = pltpu.SemaphoreType.DMA
    several = lambda count: pltpu.SemaphoreType.DMA((count,))
    grads = pl.pallas_call(
        lambda *refs: layer_kernel(seq_count, ch_count, *refs),
        in_specs=[vmem] * 9,
        out_specs=[vmem] * 4,
        out_shape=[jax.ShapeDtypeStruct((tokens, channels), jnp.bfloat16)] * 3
        + [jax.ShapeDtypeStruct((tokens, channels // ch_count), jnp.float32)],
        scratch_shapes=[
            whole(ch_count * jobs), part(ch_count * far_jobs), part(jobs), whole(ch_count * slots), part(slots), part(slots),
            whole(ch_count * slots), part(slots), part(slots), whole(ch_count * jobs), part(ch_count * far_jobs), part(jobs), part(far_jobs),
            lines, lines, spectrum, spectrum, spectrum, spectrum,
            single, single, single, single,
            several(LOCAL_SLOTS), several(JOB_SLOTS), several(LOCAL_SLOTS),
            single, single, single,
            several(JOB_SLOTS), several(JOB_SLOTS), several(JOB_SLOTS), several(JOB_SLOTS),
        ],
        compiler_params=pltpu.CompilerParams(vmem_limit_bytes=VMEM_LIMIT, collective_id=0, has_side_effects=True),
        name="layer",
    )(query_gate[0], key_input[0], value_input[0], grad_output[0], filter_raw, skip_gain[None], *tables(seq_count, tokens))
    return (grads[0][None], grads[1][None], grads[2][None], grads[3])


def solution(mesh):
    in_specs = (
        P("ch", "seq", None),
        P("ch", "seq", None),
        P("ch", "seq", None),
        P("ch", "seq", None),
        P("seq", None),
        P(),
    )
    out_specs = (P("ch", "seq", None), P("ch", "seq", None), P("ch", "seq", None), P("seq", "ch"))

    def body(*arrays):
        seq_count, ch_count = mesh.shape["seq"], mesh.shape["ch"]
        _, tokens, channels = arrays[0].shape
        fits = ch_count == 2 and tokens == LANES and seq_count == PLANES * QUARTERS and channels == ch_count * len(PLAN) * LANES
        return (fast_shards if fits else shards)(*arrays)

    return jax.shard_map(body, mesh=mesh, in_specs=in_specs, out_specs=out_specs, check_vma=False)
```

time: 131 us -> 129 us (0.985)
  no operation moved by 1% of the time
where the time goes in v1:
time: 129 us
  Pallas kernels  123 us (95%)
  local copies, waits for them, and re-layouts  5.19 us (4%)
    pallas_call x1, Pallas kernels, fast_shards(): pl.pallas_call(lambda *refs: layer_kernel(seq_count, ch_count, *refs), in...  123 us
    unnamed x10, local copies, waits for them, and re-layouts  5.19 us

profile of v1, /device:TPU:16, one launch (start us, length us, event | category | flops | bytes accessed | tf_op | source)
XLA Modules:
  0.0 129.0 jit_solution(532853647922614433)
XLA Ops:
  0.6 123.2 %layer.1 = (bf16[128,2048]{1,0:T(8,128)(2,1)}, bf16[128,2048]{1,0:T(8,128)(2,1)}, bf16[128,2048]{1,0:T(8,128)(2,1)}, f32[128,1024]{1,0:T(8,128)}) custom-call(bf16[128,2048]{1,0:T(8,128)(2,1)} %bitcast.8, bf16[128,2048]{1,0:T(8,128)(2,1)} %bitcast.9, bf16[128,2048]{1,0:T(8,128)(2,1)} %bitcast.10, bf16[128,2048]{1,0:T(8,128)(2,1)} %bitcast.11, ...), custom_call_target="tpu_custom_call" | custom-call | tf_op jit(solution)/shard_map/layer/pallas_call | solution.py:760
  123.8 0.0 copy-start.2
  123.8 1.9 %copy.17 = bf16[1,128,2048]{2,1,0:T(8,128)(2,1)} copy(bf16[1,128,2048]{2,1,0:T(8,128)(2,1)} %bitcast.14) | data formatting | bytes 1048576
  125.8 0.0 copy-done.2
  125.8 0.0 copy-start.1
  125.8 0.8 copy.18
  126.6 0.4 copy-done.1
  127.0 0.0 copy-start
  127.0 0.8 copy.19
  127.8 0.4 copy-done
  128.2 0.8 copy.20
Async XLA Ops:
  123.8 2.0 %copy-start.2 = (bf16[128,2048]{1,0:T(8,128)(2,1)S(1)}, bf16[128,2048]{1,0:T(8,128)(2,1)}, u32[]{:S(2)}) copy-start(bf16[128,2048]{1,0:T(8,128)(2,1)} %get-tuple-element.9) | copy-start | bytes 1572868
  125.8 1.2 copy-start.1
  127.0 1.2 copy-start

commit v2 on v1

--- a/solution.py
+++ b/solution.py
@@ -211,6 +211,7 @@
 PLAN_STEP = 3
 JOB_SLOTS = 3
 LOCAL_SLOTS = 5
+AT_ONCE = 2
 
 
 def left_mask(shape):
@@ -251,6 +252,15 @@
 
 def offsets(count):
     return sorted(range(count), key=lambda step: abs(2 * step - count))
+
+
+def repeat(first, count, at_once, body):
+    def several(index, carry):
+        for inner in range(at_once):
+            body(first + index * at_once + inner)
+        return carry
+
+    lax.fori_loop(0, (count - first) // at_once, several, 0)
 
 
 def greet_all(seq_count, ch_count, me_seq, me_ch):
@@ -316,17 +326,14 @@
         lanes = pl.ds(pl.multiple_of(side * side_channels + group * LANES, LANES), LANES)
         base = side * jobs + QUARTERS * group
 
-        def body(chunk, carry):
+        for chunk in range(half_tokens // 16):
             pieces = []
-            rows = [pl.ds(pl.multiple_of(chunk * 16 + first, 16), 16) for first in (0, half_tokens)]
+            rows = [pl.ds(chunk * 16 + first, 16) for first in (0, half_tokens)]
             for one, two in ((key_ref, value_ref), (out_ref, query_ref)):
                 for at in rows:
                     pieces.append(one[at, lanes].astype(jnp.float32) * two[at, lanes].astype(jnp.float32))
             for index, piece in enumerate(transpose_quarters(pieces)):
                 send[base + index, rows[0], :] = piece
-            return carry
-
-        lax.fori_loop(0, half_tokens // 16, body, 0)
 
     def halve(group, side):
         far = group - 1 - lax.div(group, PLAN_STEP)
@@ -471,56 +478,60 @@
         forward = (fwd_ref[0], fwd_ref[1])
         inverse = (inv_ref[0], inv_ref[1])
 
-        def middle(k, carry):
-            cosine, sine = tw_scr[stride * k, 0], tw_scr[stride * k, 1]
-            real, imag = spec[k, 0], spec[k, 1]
-            real, imag = real * cosine + imag * sine, imag * cosine - real * sine
-            tr, ti = taps_spec[k, 0], taps_spec[k, 1]
-            tr, ti = tr * cosine + ti * sine, ti * cosine - tr * sine
-            real, imag = across(forward, jnp.concatenate([real, tr], axis=1), jnp.concatenate([imag, ti], axis=1))
-            h_r, h_i = real[:, LANES:], imag[:, LANES:]
-            a_r, a_i = real[:, :LANES], imag[:, :LANES]
-            h_i = jnp.where(left_mask(h_i.shape), h_i, -h_i)
-            g_r, g_i = swap_halves(a_r), swap_halves(a_i)
-            c_r, c_i = a_r * g_r + a_i * g_i, a_r * g_i - a_i * g_r
-            p_r, p_i = a_r * h_r - a_i * h_i, a_r * h_i + a_i * h_r
-            weight = jnp.where((k == 0) | (k == blocks), 0.5 / (blocks * tokens), 1.0 / (blocks * tokens))
-            cosine, sine = cosine * weight, sine * weight
-            both_r, both_i = across(inverse, jnp.concatenate([p_r, c_r], axis=1), jnp.concatenate([p_i, c_i], axis=1))
-            br, bi = both_r[:, :LANES], both_i[:, :LANES]
-            cr, ci = both_r[:, LANES:], both_i[:, LANES:]
-            spec[k, 0] = br * cosine - bi * sine
-            spec[k, 1] = bi * cosine + br * sine
-            corr_spec[k, 0] = cr * cosine - ci * sine
-            corr_spec[k, 1] = ci * cosine + cr * sine
+        def middle(index, carry):
+            ks = [index * AT_ONCE + inner for inner in range(AT_ONCE)]
+            turns_at = [(tw_scr[stride * k, 0], tw_scr[stride * k, 1]) for k in ks]
+            reals, imags = [], []
+            for k, (cosine, sine) in zip(ks, turns_at):
+                for held in (spec, taps_spec):
+                    real, imag = held[k, 0], held[k, 1]
+                    reals.append(real * cosine + imag * sine)
+                    imags.append(imag * cosine - real * sine)
+            real, imag = across(forward, jnp.concatenate(reals, axis=1), jnp.concatenate(imags, axis=1))
+            reals, imags = [], []
+            for inner in range(AT_ONCE):
+                first = 2 * LANES * inner
+                a_r, a_i = real[:, first:first + LANES], imag[:, first:first + LANES]
+                h_r, h_i = real[:, first + LANES:first + 2 * LANES], imag[:, first + LANES:first + 2 * LANES]
+                h_i = jnp.where(left_mask(h_i.shape), h_i, -h_i)
+                g_r, g_i = swap_halves(a_r), swap_halves(a_i)
+                reals += [a_r * h_r - a_i * h_i, a_r * g_r + a_i * g_i]
+                imags += [a_r * h_i + a_i * h_r, a_r * g_i - a_i * g_r]
+            real, imag = across(inverse, jnp.concatenate(reals, axis=1), jnp.concatenate(imags, axis=1))
+            for inner, (k, (cosine, sine)) in enumerate(zip(ks, turns_at)):
+                weight = jnp.where((k == 0) | (k == blocks), 0.5 / (blocks * tokens), 1.0 / (blocks * tokens))
+                cosine, sine = cosine * weight, sine * weight
+                for side, held in enumerate((spec, corr_spec)):
+                    first = LANES * (2 * inner + side)
+                    br, bi = real[:, first:first + LANES], imag[:, first:first + LANES]
+                    held[k, 0] = br * cosine - bi * sine
+                    held[k, 1] = bi * cosine + br * sine
             return carry
 
-        lax.fori_loop(0, blocks + 1, middle, 0)
+        lax.fori_loop(0, blocks // AT_ONCE + 1, middle, 0)
         synthesise(spec, lines, blocks)
         synthesise(corr_spec, taps_lines, blocks)
 
     def open_taps(slot, blocks):
-        def body(n, carry):
+        def body(n):
             packed = taps_recv[slot * blocks + n]
             turned = [turn_quarters(packed, count) for count in range(QUARTERS)]
             for k in range(QUARTERS):
                 taps_lines[n, part_tokens * k:part_tokens * (k + 1), :] = choose_quarters([turned[(u - k) % QUARTERS] for u in range(QUARTERS)])
-            return carry
-
-        lax.fori_loop(0, blocks, body, 0)
+
+        repeat(0, blocks, 8, body)
 
     def open_whole(slot, blocks, first):
-        def body(n, carry):
+        def body(n):
             base = slot * ch_count * blocks + n
             top, bottom = interleave(recv[base], recv[base + blocks])
             lines[n, :half_tokens, :] = top
             lines[n, half_tokens:, :] = bottom
-            return carry
-
-        lax.fori_loop(first, blocks, body, 0)
+
+        repeat(first, blocks, 4, body)
 
     def open_half(slot):
-        def body(n, carry):
+        def body(n):
             one, two = recv_half[slot * seq_count + n], recv_half[slot * seq_count + half_seq + n]
             left = left_mask(one.shape)
             for first in (0, part_tokens):
@@ -528,39 +539,35 @@
                 lines[n, first:first + part_tokens, :] = jnp.where(left, top, 0.0)
                 lines[n, half_tokens + first:half_tokens + first + part_tokens, :] = jnp.where(left, bottom, 0.0)
                 one, two = swap_halves(one), swap_halves(two)
-            return carry
-
-        lax.fori_loop(0, half_seq, body, 0)
+
+        repeat(0, half_seq, 4, body)
 
     def close_whole(slot, blocks, first):
-        def body(n, carry):
+        def body(n):
             base = slot * ch_count * blocks + n
             one, two = interleave(lines[n, :half_tokens, :], lines[n, half_tokens:, :])
             result[base] = one
             result[base + blocks] = two
-            return carry
-
-        lax.fori_loop(first, blocks, body, 0)
+
+        repeat(first, blocks, 4, body)
 
     def close_half(slot):
-        def body(n, carry):
+        def body(n):
             for index, piece in enumerate(interleave(lines[n, :half_tokens, :], lines[n, half_tokens:, :])):
                 top, bottom = piece[:part_tokens], piece[part_tokens:]
                 result_half[slot * seq_count + index * half_seq + n] = jnp.where(left_mask(top.shape), swap_halves(bottom), top)
-            return carry
-
-        lax.fori_loop(0, half_seq, body, 0)
+
+        repeat(0, half_seq, 4, body)
 
     def close_corr(slot, blocks):
-        def body(n, carry):
+        def body(n):
             pieces = []
             for k in range(QUARTERS):
                 piece = taps_lines[n, part_tokens * k:part_tokens * (k + 1), :]
                 pieces.append(turn_quarters((piece + turn_quarters(piece, -1)) * scale, k))
             corr_result[slot * blocks + n] = choose_quarters(pieces)
-            return carry
-
-        lax.fori_loop(0, blocks, body, 0)
+
+        repeat(0, blocks, 4, body)
 
     def deliver(slot, blocks, group, first, count):
         job = QUARTERS * group + place
@@ -650,8 +657,8 @@
         base = side * jobs + QUARTERS * group
         skip = skip_ref[:, lanes]
 
-        def body(chunk, carry):
-            rows = [pl.ds(pl.multiple_of(chunk * 16 + first, 16), 16) for first in (0, half_tokens)]
+        for chunk in range(half_tokens // 16):
+            rows = [pl.ds(chunk * 16 + first, 16) for first in (0, half_tokens)]
             pieces = transpose_quarters([back[base + index, rows[0], :] for index in range(QUARTERS)])
             for at, conv, behind in zip(rows, pieces[:2], pieces[2:]):
                 query_f = query_ref[at, lanes].astype(jnp.float32)
@@ -663,9 +670,6 @@
                 gq_ref[at, lanes] = (out_f * conv).astype(jnp.bfloat16)
                 gk_ref[at, lanes] = (behind * value_f).astype(jnp.bfloat16)
                 gv_ref[at, lanes] = (behind * key_f).astype(jnp.bfloat16)
-            return carry
-
-        lax.fori_loop(0, half_tokens // 16, body, 0)
 
     def finish_corr(group):
         lanes = pl.ds(pl.multiple_of(group * LANES, LANES), LANES)
@@ -752,7 +756,8 @@
     far_jobs = QUARTERS * LOCAL_SLOTS
     whole = lambda count: pltpu.VMEM((count, tokens // 2, LANES), jnp.float32)
     part = lambda count: pltpu.VMEM((count, tokens // QUARTERS, LANES), jnp.float32)
-    spectrum = pltpu.VMEM((seq_count + 1, 2, tokens, LANES), jnp.float32)
+    spectrum = pltpu.VMEM((seq_count + AT_ONCE, 2, tokens, LANES), jnp.float32)
+    turning = pltpu.VMEM((seq_count + 2 * AT_ONCE, 2, tokens, LANES), jnp.float32)
     lines = pltpu.VMEM((seq_count, tokens, LANES), jnp.float32)
     slots = JOB_SLOTS * seq_count
     single = pltpu.SemaphoreType.DMA
@@ -766,7 +771,7 @@
         scratch_shapes=[
             whole(ch_count * jobs), part(ch_count * far_jobs), part(jobs), whole(ch_count * slots), part(slots), part(slots),
             whole(ch_count * slots), part(slots), part(slots), whole(ch_count * jobs), part(ch_count * far_jobs), part(jobs), part(far_jobs),
-            lines, lines, spectrum, spectrum, spectrum, spectrum,
+            lines, lines, spectrum, spectrum, spectrum, turning,
             single, single, single, single,
             several(LOCAL_SLOTS), several(JOB_SLOTS), several(LOCAL_SLOTS),
             single, single, single,

time: 129 us -> 104 us (0.81)
  Pallas kernels: 123 us -> 97.5 us
    pallas_call x1, Pallas kernels: 123 us -> 97.5 us  [fast_shards(): pl.pallas_call(lambda *refs: layer_kernel(seq_count, ch_count, *refs), in...]
where the time goes in v2:
time: 104 us; the launch traced here: 103 us
  Pallas kernels  97.5 us (94%)
  local copies, waits for them, and re-layouts  5.19 us (5%)
    pallas_call x1, Pallas kernels, fast_shards(): pl.pallas_call(lambda *refs: layer_kernel(seq_count, ch_count, *refs), in...  97.5 us
    unnamed x10, local copies, waits for them, and re-layouts  5.19 us

profile of v2, /device:TPU:16, one launch (start us, length us, event | category | flops | bytes accessed | tf_op | source)
XLA Modules:
  0.0 103.4 jit_solution(13364328575278191206)
XLA Ops:
  0.6 97.5 %layer.1 = (bf16[128,2048]{1,0:T(8,128)(2,1)}, bf16[128,2048]{1,0:T(8,128)(2,1)}, bf16[128,2048]{1,0:T(8,128)(2,1)}, f32[128,1024]{1,0:T(8,128)}) custom-call(bf16[128,2048]{1,0:T(8,128)(2,1)} %bitcast.8, bf16[128,2048]{1,0:T(8,128)(2,1)} %bitcast.9, bf16[128,2048]{1,0:T(8,128)(2,1)} %bitcast.10, bf16[128,2048]{1,0:T(8,128)(2,1)} %bitcast.11, ...), custom_call_target="tpu_custom_call" | custom-call | tf_op jit(solution)/shard_map/layer/pallas_call | solution.py:765
  98.2 0.0 copy-start.2
  98.2 1.9 %copy.17 = bf16[1,128,2048]{2,1,0:T(8,128)(2,1)} copy(bf16[1,128,2048]{2,1,0:T(8,128)(2,1)} %bitcast.14) | data formatting | bytes 1048576
  100.1 0.0 copy-done.2
  100.1 0.0 copy-start.1
  100.1 0.8 copy.18
  100.9 0.4 copy-done.1
  101.4 0.0 copy-start
  101.4 0.8 copy.19
  102.2 0.4 copy-done
  102.6 0.8 copy.20
Async XLA Ops:
  98.2 2.0 %copy-start.2 = (bf16[128,2048]{1,0:T(8,128)(2,1)S(1)}, bf16[128,2048]{1,0:T(8,128)(2,1)}, u32[]{:S(2)}) copy-start(bf16[128,2048]{1,0:T(8,128)(2,1)} %get-tuple-element.9) | copy-start | bytes 1572868
  100.1 1.2 %copy-start.1 = (bf16[128,2048]{1,0:T(8,128)(2,1)S(1)}, bf16[128,2048]{1,0:T(8,128)(2,1)}, u32[]{:S(2)}) copy-start(bf16[128,2048]{1,0:T(8,128)(2,1)} %get-tuple-element.10) | copy-start | bytes 1572868
  101.4 1.2 %copy-start = (f32[128,1024]{1,0:T(8,128)S(1)}, f32[128,1024]{1,0:T(8,128)}, u32[]{:S(2)}) copy-start(f32[128,1024]{1,0:T(8,128)} %get-tuple-element.19) | copy-start | bytes 1572868

commit v3 on v2

--- a/solution.py
+++ b/solution.py
@@ -275,8 +275,9 @@
 
 def layer_kernel(
     seq_count, ch_count,
-    query_ref, key_ref, value_ref, out_ref, filter_ref, skip_ref, fwd_ref, inv_ref, tw_ref,
+    query_hbm, key_hbm, value_hbm, out_hbm, filter_hbm, skip_hbm, fwd_hbm, inv_hbm, tw_hbm,
     gq_ref, gk_ref, gv_ref, gf_ref,
+    query_ref, key_ref, value_ref, out_ref, filter_ref, skip_ref, fwd_ref, inv_ref, tw_ref, load_sem,
     send, send_half, taps_send, recv, recv_half, taps_recv,
     result, result_half, corr_result, back, back_half, corr, corr_far,
     lines, taps_lines, spec, taps_spec, corr_spec, tw_scr,
@@ -301,6 +302,15 @@
     own = [[group for group, (at, owner) in enumerate(PLAN) if owner == p] for p in range(PLANES)]
     own[0] = far_groups
     kept = [len(groups) for groups in own]
+    loads = [
+        pltpu.make_async_copy(source, target, load_sem.at[index])
+        for index, (source, target) in enumerate((
+            (key_hbm, key_ref), (value_hbm, value_ref), (out_hbm, out_ref), (query_hbm, query_ref), (filter_hbm, filter_ref),
+            (tw_hbm, tw_ref), (fwd_hbm, fwd_ref), (inv_hbm, inv_ref), (skip_hbm, skip_ref),
+        ))
+    ]
+    for load in loads:
+        load.start()
     barrier = greet_all(seq_count, ch_count, me_seq, me_ch)
 
     def start(source, target, seq, ch, send_at, recv_at):
@@ -433,6 +443,8 @@
             halve(group, 0)
             halve(group, 1)
 
+    for load in loads[:5]:
+        load.wait()
     ready(0)
     pl.semaphore_wait(barrier, seq_count * ch_count - 1)
 
@@ -443,6 +455,8 @@
         return carry
 
     lax.fori_loop(0, len(PLAN), feed, 0)
+    for load in loads[5:]:
+        load.wait()
     for k in range(seq_count + 1):
         for part in range(2):
             tw_scr[k, part] = jnp.broadcast_to(tw_ref[part, :, k:k + 1], (tokens, LANES))
@@ -748,6 +762,15 @@
     return pieces(forward), pieces(inverse), twiddle
 
 
+def hand_out(*refs):
+    count = len(refs) // 2
+    copies = [pltpu.make_async_copy(refs[i], refs[count + i], refs[-1].at[i]) for i in range(count)]
+    for copy in copies:
+        copy.start()
+    for copy in copies:
+        copy.wait()
+
+
 def fast_shards(query_gate, key_input, value_input, grad_output, filter_raw, skip_gain):
     seq_count, ch_count = lax.axis_size("seq"), lax.axis_size("ch")
     _, tokens, channels = key_input.shape
@@ -762,13 +785,13 @@
     slots = JOB_SLOTS * seq_count
     single = pltpu.SemaphoreType.DMA
     several = lambda count: pltpu.SemaphoreType.DMA((count,))
+    inputs = (query_gate[0], key_input[0], value_input[0], grad_output[0], filter_raw, skip_gain[None], *tables(seq_count, tokens))
     grads = pl.pallas_call(
         lambda *refs: layer_kernel(seq_count, ch_count, *refs),
-        in_specs=[vmem] * 9,
+        in_specs=[pl.BlockSpec(memory_space=pltpu.HBM)] * len(inputs),
         out_specs=[vmem] * 4,
-        out_shape=[jax.ShapeDtypeStruct((tokens, channels), jnp.bfloat16)] * 3
-        + [jax.ShapeDtypeStruct((tokens, channels // ch_count), jnp.float32)],
-        scratch_shapes=[
+        out_shape=[pltpu.VMEM((tokens, channels), jnp.bfloat16)] * 3 + [pltpu.VMEM((tokens, channels // ch_count), jnp.float32)],
+        scratch_shapes=[pltpu.VMEM(array.shape, array.dtype) for array in inputs] + [several(len(inputs))] + [
             whole(ch_count * jobs), part(ch_count * far_jobs), part(jobs), whole(ch_count * slots), part(slots), part(slots),
             whole(ch_count * slots), part(slots), part(slots), whole(ch_count * jobs), part(ch_count * far_jobs), part(jobs), part(far_jobs),
             lines, lines, spectrum, spectrum, spectrum, turning,
@@ -779,7 +802,16 @@
         ],
         compiler_params=pltpu.CompilerParams(vmem_limit_bytes=VMEM_LIMIT, collective_id=0, has_side_effects=True),
         name="layer",
-    )(query_gate[0], key_input[0], value_input[0], grad_output[0], filter_raw, skip_gain[None], *tables(seq_count, tokens))
+    )(*inputs)
+    grads = pl.pallas_call(
+        hand_out,
+        in_specs=[vmem] * len(grads),
+        out_specs=[pl.BlockSpec(memory_space=pltpu.HBM)] * len(grads),
+        out_shape=[jax.ShapeDtypeStruct(array.shape, array.dtype) for array in grads],
+        scratch_shapes=[several(len(grads))],
+        compiler_params=pltpu.CompilerParams(vmem_limit_bytes=1024 * 1024),
+        name="hand_out",
+    )(*grads)
     return (grads[0][None], grads[1][None], grads[2][None], grads[3])
 
 

time: 104 us -> 97.5 us (0.938)
  local copies, waits for them, and re-layouts: 5.19 us -> 0 us
    unnamed x10 -> x0, local copies, waits for them, and re-layouts: 5.19 us -> none
    pallas_call x1, Pallas kernels: 97.5 us -> 95.4 us  [fast_shards(): pl.pallas_call(lambda *refs: layer_kernel(seq_count, ch_count, *refs), in...]
    pallas_call x0 -> x1, Pallas kernels: none -> 1.35 us  [fast_shards(): pl.pallas_call(hand_out, in_specs=[vmem] * len(grads), out_specs=[pl.Bloc...]
where the time goes in v3:
time: 97.5 us; the launch traced here: 97.4 us
  Pallas kernels  96.7 us (99%)
    pallas_call x1, Pallas kernels, fast_shards(): pl.pallas_call(lambda *refs: layer_kernel(seq_count, ch_count, *refs), in...  95.4 us

profile of v3, /device:TPU:16, one launch (start us, length us, event | category | flops | bytes accessed | tf_op | source)
XLA Modules:
  0.0 97.4 jit_solution(15088351881417870175)
XLA Ops:
  0.6 95.4 %layer.1 = (bf16[128,2048]{1,0:T(8,128)(2,1)S(1)}, bf16[128,2048]{1,0:T(8,128)(2,1)S(1)}, bf16[128,2048]{1,0:T(8,128)(2,1)S(1)}, f32[128,1024]{1,0:T(8,128)S(1)}) custom-call(bf16[128,2048]{1,0:T(8,128)(2,1)} %bitcast.8, bf16[128,2048]{1,0:T(8,128)(2,1)} %bitcast.9, bf16[128,2048]{1,0:T(8,128)(2,1)} %bitcast.10, bf16[128,2048]{1,0:T(8,128)(2,1)} %bitcast.11, ...), custom_call_target="tpu_custom_call" | custom-call | tf_op jit(solution)/shard_map/layer/pallas_call | solution.py:789
  96.0 1.3 %hand_out.1 = (bf16[128,2048]{1,0:T(8,128)(2,1)}, bf16[128,2048]{1,0:T(8,128)(2,1)}, bf16[128,2048]{1,0:T(8,128)(2,1)}, f32[128,1024]{1,0:T(8,128)}) custom-call(bf16[128,2048]{1,0:T(8,128)(2,1)S(1)} %get-tuple-element.12.refs_0_, bf16[128,2048]{1,0:T(8,128)(2,1)S(1)} %get-tuple-element.13.refs_1_, bf16[128,2048]{1,0:T(8,128)(2,1)S(1)} %get-tuple-element.14.refs_2_, ...), custom_call_target="tpu_custom_call" | custom-call | tf_op jit(solution)/shard_map/hand_out/pallas_call | solution.py:806

commit v4 on v3

--- a/solution.py
+++ b/solution.py
@@ -206,12 +206,26 @@
 
 QUARTERS = 4
 QUARTER = LANES // QUARTERS
-PLAN = ((0, 1), (0, 2), (0, 3), (1, 1), (1, 2), (1, 3), (2, 1), (2, 2))
 PLANES = 4
-PLAN_STEP = 3
-JOB_SLOTS = 3
-LOCAL_SLOTS = 5
-AT_ONCE = 2
+AT_ONCE = 6
+PLAN = (
+    (2, 0, 0, 0),
+    (3, 0, 0, 1),
+    (1, 0, None, None),
+    (2, 1, 0, 2),
+    (3, 1, 0, 3),
+    (1, 1, None, None),
+    (2, 2, 0, 4),
+    (3, 2, 1, 0),
+)
+ORDER = (0, 1, 2, 3, 4, 5, 6, 7)
+FAR = tuple(group for group, entry in enumerate(PLAN) if entry[2] is not None)
+RELAYED = ()
+OWNED = tuple(tuple(g for g, entry in enumerate(PLAN) if entry[0] == plane) for plane in range(PLANES))
+LOCAL = tuple(tuple(g for g in FAR if PLAN[g][2] == plane) for plane in range(PLANES))
+SLOTS = max(len(groups) for groups in OWNED)
+LOCAL_SLOTS = max(len(groups) for groups in LOCAL)
+NEAR_SLOTS = len(OWNED[1])
 
 
 def left_mask(shape):
@@ -280,10 +294,10 @@
     query_ref, key_ref, value_ref, out_ref, filter_ref, skip_ref, fwd_ref, inv_ref, tw_ref, load_sem,
     send, send_half, taps_send, recv, recv_half, taps_recv,
     result, result_half, corr_result, back, back_half, corr, corr_far,
-    lines, taps_lines, spec, taps_spec, corr_spec, tw_scr,
+    lines, taps_lines, spec, taps_spec, corr_spec, tw_scr, relay,
     send_sem, half_send_sem, taps_send_sem, local_taps_send_sem,
     recv_sem, half_recv_sem, taps_recv_sem,
-    back_send_sem, back_half_send_sem, corr_send_sem,
+    back_send_sem, back_half_send_sem, corr_send_sem, relay_sem, relay_taps_sem,
     back_sem, back_half_sem, corr_sem, corr_far_sem,
 ):
     me_seq, me_ch = lax.axis_index("seq"), lax.axis_index("ch")
@@ -297,11 +311,16 @@
     scale = (seq_count * tokens) ** -0.5
     side_channels = channels // ch_count
     jobs = QUARTERS * len(PLAN)
-    far_groups = [group for group, (_, owner) in enumerate(PLAN) if owner >= PLANES // 2]
-    far_jobs = QUARTERS * len(far_groups)
-    own = [[group for group, (at, owner) in enumerate(PLAN) if owner == p] for p in range(PLANES)]
-    own[0] = far_groups
-    kept = [len(groups) for groups in own]
+    far_jobs = QUARTERS * len(FAR)
+    local_whole = NEAR_SLOTS * ch_count * seq_count
+    local_part = NEAR_SLOTS * seq_count
+
+    def look(table):
+        out = 0
+        for value, known in table:
+            out = out + jnp.where(known, value, 0)
+        return out
+
     loads = [
         pltpu.make_async_copy(source, target, load_sem.at[index])
         for index, (source, target) in enumerate((
@@ -346,7 +365,7 @@
                 send[base + index, rows[0], :] = piece
 
     def halve(group, side):
-        far = group - 1 - lax.div(group, PLAN_STEP)
+        far = FAR.index(group)
         for index in range(QUARTERS):
             piece = send[side * jobs + QUARTERS * group + index]
             top, bottom = piece[:part_tokens], piece[part_tokens:]
@@ -362,10 +381,8 @@
         return [(step, turn) for step in offsets(width) for turn in reversed(range(ch_count))]
 
     def send_taps(group):
-        slot = lax.div(group, PLAN_STEP)
-        owner = 1 + lax.rem(group, PLAN_STEP)
-        far = group - 1 - slot
-        is_far = owner > 1
+        owner, slot, near_plane, near_slot = PLAN[group]
+        far = near_plane is not None
         for step in offsets(width):
             at = lax.rem(place + step, width)
             source = taps_send.at[QUARTERS * group + at]
@@ -374,45 +391,37 @@
                 start(source, taps_recv.at[slot * seq_count + me_seq], owner * width + at, me_ch, taps_send_sem, taps_recv_sem.at[slot])
 
             def to_local():
-                start(source, taps_recv.at[far * half_seq + me_seq], at, me_ch, local_taps_send_sem, taps_recv_sem.at[far])
-
-            if step:
-                to_owner()
-                pl.when(is_far & (low == 1))(to_local)
-            else:
-                pl.when(plane != owner)(to_owner)
-
-                @pl.when(plane == owner)
-                def _():
-                    taps_recv[slot * seq_count + me_seq] = taps_send[QUARTERS * group + place]
-
-                pl.when(is_far & (low == 1) & (plane != 0))(to_local)
-
-                @pl.when(is_far & (plane == 0))
-                def _():
-                    taps_recv[far * half_seq + me_seq] = taps_send[QUARTERS * group + place]
+                start(
+                    source, taps_recv.at[near_plane * local_part + near_slot * half_seq + me_seq], near_plane * width + at, me_ch,
+                    local_taps_send_sem, taps_recv_sem.at[SLOTS + near_slot],
+                )
+
+            sends = plane != owner if step == 0 else plane >= 0
+            if group in RELAYED:
+                sends = sends & (plane > 0)
+            pl.when(sends)(to_owner)
+            if far:
+                pl.when((low == 1) & (plane != near_plane) if step == 0 else low == 1)(to_local)
+
+        @pl.when(plane == owner)
+        def _():
+            taps_recv[slot * seq_count + me_seq] = taps_send[QUARTERS * group + place]
+
+        if far:
+
+            @pl.when(plane == near_plane)
+            def _():
+                taps_recv[near_plane * local_part + near_slot * half_seq + me_seq] = taps_send[QUARTERS * group + place]
 
     def send_group(group):
-        slot = lax.div(group, PLAN_STEP)
-        owner = 1 + lax.rem(group, PLAN_STEP)
-        far = group - 1 - slot
-
-        @pl.when((owner > 1) & (low == 1))
-        def _():
+        owner, slot, near_plane, near_slot = PLAN[group]
+
+        def whole(target_plane, index, sem):
             for step, turn in turns():
                 at, ch = lax.rem(place + step, width), lax.rem(me_ch + turn, ch_count)
-                start(
-                    send_half.at[ch * far_jobs + QUARTERS * far + at],
-                    recv_half.at[slot * seq_count + me_ch * half_seq + me_seq],
-                    owner * width + at, ch, half_send_sem, half_recv_sem.at[slot],
-                )
-
-        def whole(target_plane, target_slot, index):
-            for step, turn in turns():
-                at, ch = lax.rem(place + step, width), lax.rem(me_ch + turn, ch_count)
 
                 def go():
-                    start(send.at[ch * jobs + QUARTERS * group + at], recv.at[index], target_plane * width + at, ch, send_sem, recv_sem.at[target_slot])
+                    start(send.at[ch * jobs + QUARTERS * group + at], recv.at[index], target_plane * width + at, ch, send_sem, sem)
 
                 if step or turn:
                     go()
@@ -423,38 +432,54 @@
                     def _():
                         recv[index] = send[me_ch * jobs + QUARTERS * group + place]
 
-        @pl.when((owner == 1) | (high == 1))
+        if near_plane is None:
+            whole(owner, (slot * ch_count + me_ch) * seq_count + me_seq, recv_sem.at[slot])
+            return
+
+        @pl.when(plane > 0 if group in RELAYED else low == 1)
         def _():
-            whole(owner, slot, (slot * ch_count + me_ch) * seq_count + me_seq)
-
-        @pl.when((owner > 1) & (low == 1))
+            @pl.when(low == 1)
+            def _():
+                for step, turn in turns():
+                    at, ch = lax.rem(place + step, width), lax.rem(me_ch + turn, ch_count)
+                    start(
+                        send_half.at[ch * far_jobs + QUARTERS * FAR.index(group) + at],
+                        recv_half.at[slot * seq_count + me_ch * half_seq + me_seq],
+                        owner * width + at, ch, half_send_sem, half_recv_sem.at[slot],
+                    )
+
+        @pl.when(high == 1)
         def _():
-            whole(0, far, (far * ch_count + me_ch) * half_seq + me_seq)
+            whole(owner, (slot * ch_count + me_ch) * half_seq + me_seq - half_seq, recv_sem.at[slot])
+
+        @pl.when(low == 1)
+        def _():
+            index = near_plane * local_whole + (near_slot * ch_count + me_ch) * half_seq + me_seq
+            whole(near_plane, index, recv_sem.at[SLOTS + near_slot])
 
     def ready(group):
         other = lax.rem(me_ch + 1, ch_count)
         prepare_taps(group)
         prepare(group, other)
         prepare(group, me_ch)
-        slot = lax.div(group, PLAN_STEP)
-
-        @pl.when((group - PLAN_STEP * slot > 0) & (low == 1))
-        def _():
-            halve(group, 0)
-            halve(group, 1)
+
+        if group in FAR:
+            pl.when(low == 1)(lambda: halves(group))
+
+    def halves(group):
+        halve(group, 0)
+        halve(group, 1)
 
     for load in loads[:5]:
         load.wait()
     ready(0)
     pl.semaphore_wait(barrier, seq_count * ch_count - 1)
 
-    def feed(group, carry):
-        pl.when(group > 0)(lambda: ready(group))
+    for group in range(len(PLAN)):
+        if group:
+            ready(group)
         send_group(group)
         send_taps(group)
-        return carry
-
-    lax.fori_loop(0, len(PLAN), feed, 0)
     for load in loads[5:]:
         load.wait()
     for k in range(seq_count + 1):
@@ -526,19 +551,19 @@
         synthesise(spec, lines, blocks)
         synthesise(corr_spec, taps_lines, blocks)
 
-    def open_taps(slot, blocks):
+    def open_taps(first, blocks):
         def body(n):
-            packed = taps_recv[slot * blocks + n]
+            packed = taps_recv[first + n]
             turned = [turn_quarters(packed, count) for count in range(QUARTERS)]
             for k in range(QUARTERS):
                 taps_lines[n, part_tokens * k:part_tokens * (k + 1), :] = choose_quarters([turned[(u - k) % QUARTERS] for u in range(QUARTERS)])
 
         repeat(0, blocks, 8, body)
 
-    def open_whole(slot, blocks, first):
+    def open_whole(start_at, blocks, first):
         def body(n):
-            base = slot * ch_count * blocks + n
-            top, bottom = interleave(recv[base], recv[base + blocks])
+            base = start_at + n - first
+            top, bottom = interleave(recv[base], recv[base + blocks - first])
             lines[n, :half_tokens, :] = top
             lines[n, half_tokens:, :] = bottom
 
@@ -556,12 +581,12 @@
 
         repeat(0, half_seq, 4, body)
 
-    def close_whole(slot, blocks, first):
+    def close_whole(start_at, blocks, first):
         def body(n):
-            base = slot * ch_count * blocks + n
+            base = start_at + n - first
             one, two = interleave(lines[n, :half_tokens, :], lines[n, half_tokens:, :])
             result[base] = one
-            result[base + blocks] = two
+            result[base + blocks - first] = two
 
         repeat(first, blocks, 4, body)
 
@@ -573,98 +598,124 @@
 
         repeat(0, half_seq, 4, body)
 
-    def close_corr(slot, blocks):
+    def close_corr(first, blocks):
         def body(n):
             pieces = []
             for k in range(QUARTERS):
                 piece = taps_lines[n, part_tokens * k:part_tokens * (k + 1), :]
                 pieces.append(turn_quarters((piece + turn_quarters(piece, -1)) * scale, k))
-            corr_result[slot * blocks + n] = choose_quarters(pieces)
+            corr_result[first + n] = choose_quarters(pieces)
 
         repeat(0, blocks, 4, body)
 
-    def deliver(slot, blocks, group, first, count):
+    def deliver(base, corr_base, group, first, count):
         job = QUARTERS * group + place
-        at_round = lax.div(group, PLAN_STEP)
-        base = slot * ch_count * blocks
         for step in offsets(count):
-            seq = first + lax.rem(me_seq + step, count)
+            at = lax.rem(me_seq + step, count)
             for turn in range(ch_count):
                 ch = lax.rem(me_ch + turn, ch_count)
                 if step or turn:
-                    start(result.at[base + ch * blocks + seq], back.at[me_ch * jobs + job], seq, ch, back_send_sem, back_sem.at[at_round])
+                    start(result.at[base + ch * count + at], back.at[me_ch * jobs + job], first + at, ch, back_send_sem, back_sem.at[group])
             if step:
-                start(corr_result.at[slot * blocks + seq], corr.at[job], seq, me_ch, corr_send_sem, corr_sem.at[at_round])
-        back[me_ch * jobs + job] = result[base + me_ch * blocks + me_seq]
-        corr[job] = corr_result[slot * blocks + me_seq]
+                start(corr_result.at[corr_base + first + at], corr.at[job], first + at, me_ch, corr_send_sem, corr_sem.at[group])
+        back[me_ch * jobs + job] = result[base + me_ch * count + me_seq - first]
+        corr[job] = corr_result[corr_base + me_seq]
 
     def deliver_half(slot, group):
-        far = QUARTERS * (group - 1 - slot) + place
+        far = QUARTERS * look([(FAR.index(g), group == g) for g in FAR]) + place
         for step in offsets(half_seq):
             seq = lax.rem(me_seq + step, half_seq)
             for turn in range(ch_count):
                 ch = lax.rem(me_ch + turn, ch_count)
                 start(
                     result_half.at[slot * seq_count + ch * half_seq + seq], back_half.at[me_ch * far_jobs + far],
-                    seq, ch, back_half_send_sem, back_half_sem.at[slot],
+                    seq, ch, back_half_send_sem, back_half_sem.at[group],
                 )
-            start(corr_result.at[slot * seq_count + seq], corr_far.at[far], seq, me_ch, corr_send_sem, corr_far_sem.at[slot])
+            start(corr_result.at[slot * seq_count + seq], corr_far.at[far], seq, me_ch, corr_send_sem, corr_far_sem.at[group])
 
     others = seq_count * ch_count - 1
 
     def owner_job(slot, carry):
-        group = PLAN_STEP * slot + plane - 1
+        group = look([(g, (plane == PLAN[g][0]) & (slot == PLAN[g][1])) for g in range(len(PLAN))])
         arrive(taps_recv, seq_count - 1, taps_recv_sem.at[slot])
-        open_taps(slot, seq_count)
+        open_taps(slot * seq_count, seq_count)
+        near_base = slot * ch_count * seq_count
+        far_base = slot * ch_count * half_seq
 
         @pl.when(high == 0)
         def _():
             arrive(recv, others, recv_sem.at[slot])
-            open_whole(slot, seq_count, 0)
+            open_whole(near_base, seq_count, 0)
 
         @pl.when(high == 1)
         def _():
             arrive(recv_half, seq_count, half_recv_sem.at[slot])
             open_half(slot)
             arrive(recv, seq_count - 1, recv_sem.at[slot])
-            open_whole(slot, seq_count, half_seq)
+            open_whole(far_base, seq_count, half_seq)
 
         convolve(seq_count)
-        close_corr(slot, seq_count)
+        close_corr(slot * seq_count, seq_count)
 
         @pl.when(high == 0)
         def _():
-            close_whole(slot, seq_count, 0)
-            deliver(slot, seq_count, group, 0, seq_count)
+            close_whole(near_base, seq_count, 0)
+            deliver(near_base, slot * seq_count, group, 0, seq_count)
 
         @pl.when(high == 1)
         def _():
             close_half(slot)
-            close_whole(slot, seq_count, half_seq)
+            close_whole(far_base, seq_count, half_seq)
             deliver_half(slot, group)
-            deliver(slot, seq_count, group, half_seq, half_seq)
+            deliver(far_base, slot * seq_count, group, half_seq, half_seq)
 
         return carry
 
+    def local_arrive(slot):
+        arrive(taps_recv, half_seq - 1, taps_recv_sem.at[SLOTS + slot])
+        arrive(recv, seq_count - 1, recv_sem.at[SLOTS + slot])
+
     def local_job(slot, carry):
-        group = slot + 1 + lax.div(slot, 2)
-        arrive(taps_recv, half_seq - 1, taps_recv_sem.at[slot])
-        open_taps(slot, half_seq)
-        arrive(recv, seq_count - 1, recv_sem.at[slot])
-        open_whole(slot, half_seq, 0)
+        group = look([(g, (plane == PLAN[g][2]) & (slot == PLAN[g][3])) for g in FAR])
+        base = plane * local_whole + slot * ch_count * half_seq
+        part_base = plane * local_part + slot * half_seq
+        pl.when(plane == 0)(lambda: local_arrive(slot)) if RELAYED else local_arrive(slot)
+        open_taps(part_base, half_seq)
+        open_whole(base, half_seq, 0)
         convolve(half_seq)
-        close_corr(slot, half_seq)
-        close_whole(slot, half_seq, 0)
-        deliver(slot, half_seq, group, 0, half_seq)
+        close_corr(part_base, half_seq)
+        close_whole(base, half_seq, 0)
+        deliver(base, part_base, group, 0, half_seq)
         return carry
 
-    @pl.when(plane > 0)
+    def hand_on(group):
+        owner, slot, near_plane, near_slot = PLAN[group]
+        local_arrive(near_slot)
+        seq = owner * width + place
+        for n in range(width):
+            start(
+                taps_recv.at[near_plane * local_part + near_slot * half_seq + n], taps_recv.at[slot * seq_count + n],
+                seq, me_ch, relay_taps_sem, taps_recv_sem.at[slot],
+            )
+        for ch in range(ch_count):
+            for n in range(width):
+                piece = recv[near_plane * local_whole + (near_slot * ch_count + ch) * half_seq + n]
+                top, bottom = piece[:part_tokens], piece[part_tokens:]
+                relay[(near_slot * ch_count + ch) * width + n] = jnp.where(left_mask(top.shape), top, swap_halves(bottom))
+        for ch in range(ch_count):
+            for n in range(width):
+                start(
+                    relay.at[(near_slot * ch_count + ch) * width + n], recv_half.at[slot * seq_count + ch * half_seq + n],
+                    seq, me_ch, relay_sem, half_recv_sem.at[slot],
+                )
+
+    @pl.when(plane == 1)
     def _():
-        lax.fori_loop(0, JOB_SLOTS - lax.div(plane, PLANES - 1), owner_job, 0)
-
-    @pl.when(plane == 0)
-    def _():
-        lax.fori_loop(0, LOCAL_SLOTS, local_job, 0)
+        for group in RELAYED:
+            hand_on(group)
+
+    lax.fori_loop(0, look([(len(groups), plane == p) for p, groups in enumerate(OWNED)]), owner_job, 0)
+    lax.fori_loop(0, look([(len(groups), plane == p) for p, groups in enumerate(LOCAL)]), local_job, 0)
 
     def finish(group, side):
         lanes = pl.ds(pl.multiple_of(side * side_channels + group * LANES, LANES), LANES)
@@ -691,7 +742,8 @@
         for k, piece in enumerate(pieces):
             gf_ref[part_tokens * k:part_tokens * (k + 1), lanes] = piece
 
-    def join_half(far, group):
+    def join_half(group):
+        far = FAR.index(group)
         for side in range(ch_count):
             for index in range(QUARTERS):
                 piece = back_half[side * far_jobs + QUARTERS * far + index]
@@ -702,48 +754,47 @@
         for index in range(QUARTERS):
             corr[QUARTERS * group + index] += corr_far[QUARTERS * far + index]
 
-    for at_round in range(JOB_SLOTS):
-        groups = [group for group, (when, _) in enumerate(PLAN) if when == at_round]
-        for p in range(PLANES):
-            mine = sum(PLAN[group][0] == at_round for group in own[p])
-
-            @pl.when(plane == p)
+    for group in ORDER:
+        owner, _, near_plane, _ = PLAN[group]
+        mine = plane == owner
+        if near_plane is not None:
+            mine = mine | (plane == near_plane)
+        for own in (0, 1):
+
+            @pl.when(mine if own else jnp.logical_not(mine))
             def _():
-                arrive(back, QUARTERS * ch_count * len(groups) - mine, back_sem.at[at_round])
-                arrive(corr, QUARTERS * len(groups) - mine, corr_sem.at[at_round])
-
-        @pl.when(low == 1)
-        def _():
-            count = QUARTERS * sum(group in far_groups for group in groups)
-            arrive(back_half, count * ch_count, back_half_sem.at[at_round])
-            arrive(corr_far, count, corr_far_sem.at[at_round])
-            for group in groups:
-                if group in far_groups:
-                    join_half(far_groups.index(group), group)
-
-        def finish_group(index, carry):
-            group = groups[0] + index
-            finish(group, 0)
-            finish(group, 1)
-            finish_corr(group)
-            return carry
-
-        lax.fori_loop(0, len(groups), finish_group, 0)
+                arrive(back, QUARTERS * ch_count - own, back_sem.at[group])
+                arrive(corr, QUARTERS - own, corr_sem.at[group])
+
+        if near_plane is not None:
+
+            @pl.when(low == 1)
+            def _():
+                arrive(back_half, QUARTERS * ch_count, back_half_sem.at[group])
+                arrive(corr_far, QUARTERS, corr_far_sem.at[group])
+                join_half(group)
+
+        finish(group, 0)
+        finish(group, 1)
+        finish_corr(group)
 
     for p in range(PLANES):
         is_low = p < PLANES // 2
-        count = kept[p]
+        owned, local = len(OWNED[p]), len(LOCAL[p])
+        direct = len(FAR) - (0 if p else len(RELAYED))
 
         @pl.when(plane == p)
         def _():
-            depart(send, ch_count * jobs - count, send_sem)
-            depart(send_half, ch_count * far_jobs if is_low else 0, half_send_sem)
-            depart(taps_send, jobs - (count if p else 0), taps_send_sem)
-            depart(taps_send, far_jobs - (0 if p else count) if is_low else 0, local_taps_send_sem)
-            whole = (others if is_low else seq_count - 1) if p else seq_count - 1
-            depart(result, count * whole, back_send_sem)
-            depart(result_half, 0 if is_low else count * seq_count, back_half_send_sem)
-            depart(corr_result, count * ((seq_count if p else half_seq) - 1), corr_send_sem)
+            depart(send, ch_count * jobs - owned - local, send_sem)
+            depart(send_half, ch_count * QUARTERS * direct if is_low else 0, half_send_sem)
+            depart(taps_send, jobs - owned - (0 if p else QUARTERS * len(RELAYED)), taps_send_sem)
+            depart(taps_send, far_jobs - local if is_low else 0, local_taps_send_sem)
+            depart(result, owned * (others if is_low else seq_count - 1) + local * (seq_count - 1), back_send_sem)
+            depart(result_half, 0 if is_low else owned * seq_count, back_half_send_sem)
+            depart(corr_result, owned * (seq_count - 1) + local * (half_seq - 1), corr_send_sem)
+            if p == 1 and RELAYED:
+                depart(relay, len(RELAYED) * ch_count * width, relay_sem)
+                depart(taps_recv, len(RELAYED) * width, relay_taps_sem)
 
 
 def tables(seq_count, tokens):
@@ -776,13 +827,14 @@
     _, tokens, channels = key_input.shape
     vmem = pl.BlockSpec(memory_space=pltpu.VMEM)
     jobs = QUARTERS * len(PLAN)
-    far_jobs = QUARTERS * LOCAL_SLOTS
+    far_jobs = QUARTERS * len(FAR)
     whole = lambda count: pltpu.VMEM((count, tokens // 2, LANES), jnp.float32)
     part = lambda count: pltpu.VMEM((count, tokens // QUARTERS, LANES), jnp.float32)
     spectrum = pltpu.VMEM((seq_count + AT_ONCE, 2, tokens, LANES), jnp.float32)
     turning = pltpu.VMEM((seq_count + 2 * AT_ONCE, 2, tokens, LANES), jnp.float32)
     lines = pltpu.VMEM((seq_count, tokens, LANES), jnp.float32)
-    slots = JOB_SLOTS * seq_count
+    slots = SLOTS * seq_count
+    wholes = max(ch_count * NEAR_SLOTS + len(LOCAL[1]), SLOTS, LOCAL_SLOTS) * seq_count
     single = pltpu.SemaphoreType.DMA
     several = lambda count: pltpu.SemaphoreType.DMA((count,))
     inputs = (query_gate[0], key_input[0], value_input[0], grad_output[0], filter_raw, skip_gain[None], *tables(seq_count, tokens))
@@ -792,13 +844,13 @@
         out_specs=[vmem] * 4,
         out_shape=[pltpu.VMEM((tokens, channels), jnp.bfloat16)] * 3 + [pltpu.VMEM((tokens, channels // ch_count), jnp.float32)],
         scratch_shapes=[pltpu.VMEM(array.shape, array.dtype) for array in inputs] + [several(len(inputs))] + [
-            whole(ch_count * jobs), part(ch_count * far_jobs), part(jobs), whole(ch_count * slots), part(slots), part(slots),
-            whole(ch_count * slots), part(slots), part(slots), whole(ch_count * jobs), part(ch_count * far_jobs), part(jobs), part(far_jobs),
-            lines, lines, spectrum, spectrum, spectrum, turning,
+            whole(ch_count * jobs), part(ch_count * far_jobs), part(jobs), whole(wholes), part(slots), part(slots),
+            whole(wholes), part(slots), part(slots), whole(ch_count * jobs), part(ch_count * far_jobs), part(jobs), part(far_jobs),
+            lines, lines, spectrum, spectrum, spectrum, turning, part(max(len(RELAYED), 1) * seq_count // 2),
             single, single, single, single,
-            several(LOCAL_SLOTS), several(JOB_SLOTS), several(LOCAL_SLOTS),
-            single, single, single,
-            several(JOB_SLOTS), several(JOB_SLOTS), several(JOB_SLOTS), several(JOB_SLOTS),
+            several(SLOTS + LOCAL_SLOTS), several(SLOTS), several(SLOTS + LOCAL_SLOTS),
+            single, single, single, single, single,
+            several(len(PLAN)), several(len(PLAN)), several(len(PLAN)), several(len(PLAN)),
         ],
         compiler_params=pltpu.CompilerParams(vmem_limit_bytes=VMEM_LIMIT, collective_id=0, has_side_effects=True),
         name="layer",

time: 97.5 us -> 94.9 us (0.973)
  Pallas kernels: 96.7 us -> 94.1 us
    pallas_call x1, Pallas kernels: 95.4 us -> 92.8 us  [fast_shards(): pl.pallas_call(lambda *refs: layer_kernel(seq_count, ch_count, *refs), in...]
where the time goes in v4:
time: 94.9 us; the launch traced here: 94.7 us
  Pallas kernels  94.1 us (99%)
    pallas_call x1, Pallas kernels, fast_shards(): pl.pallas_call(lambda *refs: layer_kernel(seq_count, ch_count, *refs), in...  92.8 us

profile of v4, /device:TPU:16, one launch (start us, length us, event | category | flops | bytes accessed | tf_op | source)
XLA Modules:
  0.0 94.7 jit_solution(15572057595774155476)
XLA Ops:
  0.6 92.8 %layer.1 = (bf16[128,2048]{1,0:T(8,128)(2,1)S(1)}, bf16[128,2048]{1,0:T(8,128)(2,1)S(1)}, bf16[128,2048]{1,0:T(8,128)(2,1)S(1)}, f32[128,1024]{1,0:T(8,128)S(1)}) custom-call(bf16[128,2048]{1,0:T(8,128)(2,1)} %bitcast.8, bf16[128,2048]{1,0:T(8,128)(2,1)} %bitcast.9, bf16[128,2048]{1,0:T(8,128)(2,1)} %bitcast.10, bf16[128,2048]{1,0:T(8,128)(2,1)} %bitcast.11, ...), custom_call_target="tpu_custom_call" | custom-call | tf_op jit(solution)/shard_map/layer/pallas_call | solution.py:841
  93.4 1.3 %hand_out.1 = (bf16[128,2048]{1,0:T(8,128)(2,1)}, bf16[128,2048]{1,0:T(8,128)(2,1)}, bf16[128,2048]{1,0:T(8,128)(2,1)}, f32[128,1024]{1,0:T(8,128)}) custom-call(bf16[128,2048]{1,0:T(8,128)(2,1)S(1)} %get-tuple-element.12.refs_0_, bf16[128,2048]{1,0:T(8,128)(2,1)S(1)} %get-tuple-element.13.refs_1_, bf16[128,2048]{1,0:T(8,128)(2,1)S(1)} %get-tuple-element.14.refs_2_, ...), custom_call_target="tpu_custom_call" | custom-call | tf_op jit(solution)/shard_map/hand_out/pallas_call | solution.py:858

commit v5 on v4

--- a/solution.py
+++ b/solution.py
@@ -208,6 +208,7 @@
 QUARTER = LANES // QUARTERS
 PLANES = 4
 AT_ONCE = 6
+LATE = 2
 PLAN = (
     (2, 0, 0, 0),
     (3, 0, 0, 1),
@@ -413,27 +414,27 @@
             def _():
                 taps_recv[near_plane * local_part + near_slot * half_seq + me_seq] = taps_send[QUARTERS * group + place]
 
+    def whole(group, target_plane, index, sem):
+        for step, turn in turns():
+            at, ch = lax.rem(place + step, width), lax.rem(me_ch + turn, ch_count)
+
+            def go():
+                start(send.at[ch * jobs + QUARTERS * group + at], recv.at[index], target_plane * width + at, ch, send_sem, sem)
+
+            if step or turn:
+                go()
+            else:
+                pl.when(plane != target_plane)(go)
+
+                @pl.when(plane == target_plane)
+                def _():
+                    recv[index] = send[me_ch * jobs + QUARTERS * group + place]
+
     def send_group(group):
         owner, slot, near_plane, near_slot = PLAN[group]
 
-        def whole(target_plane, index, sem):
-            for step, turn in turns():
-                at, ch = lax.rem(place + step, width), lax.rem(me_ch + turn, ch_count)
-
-                def go():
-                    start(send.at[ch * jobs + QUARTERS * group + at], recv.at[index], target_plane * width + at, ch, send_sem, sem)
-
-                if step or turn:
-                    go()
-                else:
-                    pl.when(plane != target_plane)(go)
-
-                    @pl.when(plane == target_plane)
-                    def _():
-                        recv[index] = send[me_ch * jobs + QUARTERS * group + place]
-
         if near_plane is None:
-            whole(owner, (slot * ch_count + me_ch) * seq_count + me_seq, recv_sem.at[slot])
+            whole(group, owner, (slot * ch_count + me_ch) * seq_count + me_seq, recv_sem.at[slot])
             return
 
         @pl.when(plane > 0 if group in RELAYED else low == 1)
@@ -450,12 +451,15 @@
 
         @pl.when(high == 1)
         def _():
-            whole(owner, (slot * ch_count + me_ch) * half_seq + me_seq - half_seq, recv_sem.at[slot])
+            whole(group, owner, (slot * ch_count + me_ch) * half_seq + me_seq - half_seq, recv_sem.at[slot])
+
+    def send_local(group):
+        owner, slot, near_plane, near_slot = PLAN[group]
 
         @pl.when(low == 1)
         def _():
             index = near_plane * local_whole + (near_slot * ch_count + me_ch) * half_seq + me_seq
-            whole(near_plane, index, recv_sem.at[SLOTS + near_slot])
+            whole(group, near_plane, index, recv_sem.at[SLOTS + near_slot])
 
     def ready(group):
         other = lax.rem(me_ch + 1, ch_count)
@@ -478,8 +482,13 @@
     for group in range(len(PLAN)):
         if group:
             ready(group)
+        send_taps(group)
         send_group(group)
-        send_taps(group)
+        if group - LATE in FAR:
+            send_local(group - LATE)
+    for group in range(len(PLAN) - LATE, len(PLAN)):
+        if group in FAR:
+            send_local(group)
     for load in loads[5:]:
         load.wait()
     for k in range(seq_count + 1):

time: 94.9 us -> 93.6 us (0.986)
  Pallas kernels: 94.1 us -> 92.8 us
    pallas_call x1, Pallas kernels: 92.8 us -> 91.4 us  [fast_shards(): pl.pallas_call(lambda *refs: layer_kernel(seq_count, ch_count, *refs), in...]
where the time goes in v5:
time: 93.6 us; the launch traced here: 93.4 us
  Pallas kernels  92.8 us (99%)
    pallas_call x1, Pallas kernels, fast_shards(): pl.pallas_call(lambda *refs: layer_kernel(seq_count, ch_count, *refs), in...  91.4 us

profile of v5, /device:TPU:16, one launch (start us, length us, event | category | flops | bytes accessed | tf_op | source)
XLA Modules:
  0.0 93.4 jit_solution(384094532063287560)
XLA Ops:
  0.6 91.4 %layer.1 = (bf16[128,2048]{1,0:T(8,128)(2,1)S(1)}, bf16[128,2048]{1,0:T(8,128)(2,1)S(1)}, bf16[128,2048]{1,0:T(8,128)(2,1)S(1)}, f32[128,1024]{1,0:T(8,128)S(1)}) custom-call(bf16[128,2048]{1,0:T(8,128)(2,1)} %bitcast.8, bf16[128,2048]{1,0:T(8,128)(2,1)} %bitcast.9, bf16[128,2048]{1,0:T(8,128)(2,1)} %bitcast.10, bf16[128,2048]{1,0:T(8,128)(2,1)} %bitcast.11, ...), custom_call_target="tpu_custom_call" | custom-call | tf_op jit(solution)/shard_map/layer/pallas_call | solution.py:850
  92.1 1.3 %hand_out.1 = (bf16[128,2048]{1,0:T(8,128)(2,1)}, bf16[128,2048]{1,0:T(8,128)(2,1)}, bf16[128,2048]{1,0:T(8,128)(2,1)}, f32[128,1024]{1,0:T(8,128)}) custom-call(bf16[128,2048]{1,0:T(8,128)(2,1)S(1)} %get-tuple-element.12.refs_0_, bf16[128,2048]{1,0:T(8,128)(2,1)S(1)} %get-tuple-element.13.refs_1_, bf16[128,2048]{1,0:T(8,128)(2,1)S(1)} %get-tuple-element.14.refs_2_, ...), custom_call_target="tpu_custom_call" | custom-call | tf_op jit(solution)/shard_map/hand_out/pallas_call | solution.py:867

commit v6 on v5

--- a/solution.py
+++ b/solution.py
@@ -674,8 +674,8 @@
         @pl.when(high == 1)
         def _():
             close_half(slot)
+            deliver_half(slot, group)
             close_whole(far_base, seq_count, half_seq)
-            deliver_half(slot, group)
             deliver(far_base, slot * seq_count, group, half_seq, half_seq)
 
         return carry

time: 93.6 us -> 93.3 us (level)
  no operation moved by 1% of the time
where the time goes in v6:
time: 93.3 us; the launch traced here: 93.2 us
  Pallas kernels  92.5 us (99%)
    pallas_call x1, Pallas kernels, fast_shards(): pl.pallas_call(lambda *refs: layer_kernel(seq_count, ch_count, *refs), in...  91.2 us

profile of v6, /device:TPU:16, one launch (start us, length us, event | category | flops | bytes accessed | tf_op | source)
XLA Modules:
  0.0 93.2 jit_solution(7270807687885624037)
XLA Ops:
  0.6 91.2 %layer.1 = (bf16[128,2048]{1,0:T(8,128)(2,1)S(1)}, bf16[128,2048]{1,0:T(8,128)(2,1)S(1)}, bf16[128,2048]{1,0:T(8,128)(2,1)S(1)}, f32[128,1024]{1,0:T(8,128)S(1)}) custom-call(bf16[128,2048]{1,0:T(8,128)(2,1)} %bitcast.8, bf16[128,2048]{1,0:T(8,128)(2,1)} %bitcast.9, bf16[128,2048]{1,0:T(8,128)(2,1)} %bitcast.10, bf16[128,2048]{1,0:T(8,128)(2,1)} %bitcast.11, ...), custom_call_target="tpu_custom_call" | custom-call | tf_op jit(solution)/shard_map/layer/pallas_call | solution.py:850
  91.8 1.3 %hand_out.1 = (bf16[128,2048]{1,0:T(8,128)(2,1)}, bf16[128,2048]{1,0:T(8,128)(2,1)}, bf16[128,2048]{1,0:T(8,128)(2,1)}, f32[128,1024]{1,0:T(8,128)}) custom-call(bf16[128,2048]{1,0:T(8,128)(2,1)S(1)} %get-tuple-element.12.refs_0_, bf16[128,2048]{1,0:T(8,128)(2,1)S(1)} %get-tuple-element.13.refs_1_, bf16[128,2048]{1,0:T(8,128)(2,1)S(1)} %get-tuple-element.14.refs_2_, ...), custom_call_target="tpu_custom_call" | custom-call | tf_op jit(solution)/shard_map/hand_out/pallas_call | solution.py:867
